TPU v7x, 256 devices: a whole 4x4x8 slice. The times are simulated.
256 devices in a mesh: expert: 64 (over y, z_hi, x, core), group: 4 (over z_lo).
Axes of the slice: x: 4, y: 4, z: 8 (z_hi: 2, z_lo: 4; z = z_hi * 4 + z_lo), core: 2. Of those that a mesh axis runs over, the one named last changes fastest.
Arguments:
- tokens: bfloat16 [30720, 4096], P('expert', 'group'), may hold values from -6 to 6
- cotangent: bfloat16 [30720, 1024], P('expert'), may hold values from -6 to 6
- routing: int32 [30720, 1], P('expert'), may hold values from 0 to 63; in each aligned block of 480 rows (0 to 479, 480 to 959, ...) at most 15 rows name the same one
- stat_prev: float32 [64, 1024, 1024], P('expert', 'group'), as said below
- root_prev: bfloat16 [64, 1024, 1024], P('expert', 'group'), may hold values from -0.1875 to 0.1875
- owner_map: int32 [64], replicated, may hold values from 0 to 16, as said below
Outputs:
- statistic: float32 [64, 1024, 1024], P('expert', 'group')
- roots: bfloat16 [64, 1024, 1024], P('expert', 'group')
- update: bfloat16 [64, 4096, 1024], P('expert', 'group')
Inputs may be any that keep to these rules, and one draw needn't show every extreme that they name: `routing`: in the rows of one device (aligned blocks of 480 rows) no expert is named more than 15 times, a bound that some block reaches. `owner_map`: A value below 16 names the index of expert that owns this expert's statistic; the value 16 marks a statistic that is not refreshed. Exactly 16 experts are refreshed; no owner holds more than 4 of them, and some owner holds exactly 4. `stat_prev`: each expert's block is symmetric and positive definite.
All inputs are finite; a program needn't handle non-finite values.
Results may differ from a plain program's by a relative error of at most 0.0055.
Values may be sent and summed in bfloat16 or wider, within the bound.
No kernel may reach another device: no remote copies, remote signals or barrier semaphores. Data moves between devices by JAX's collectives and lax.ppermute only.
A program may use at most 64 MiB of HBM per device.

v0:
```python
import math

import jax
import jax.numpy as jnp
from jax import lax
from jax.sharding import PartitionSpec as P

ITERS = 2
POWER = 8


keep_share = 0.9


def in_one_piece(arrays, axis, split_dim, concat_dim, along):
    widths = [a.shape[along] for a in arrays]
    both = jnp.concatenate(arrays, axis=along)
    whole = lax.all_to_all(both, axis, split_axis=split_dim, concat_axis=concat_dim, tiled=True)
    return tuple(jnp.split(whole, [sum(widths[:k]) for k in range(1, len(widths))], axis=along))


def in_blocks(x, dim, peers):
    before, after = (x.shape[:dim], x.shape[dim + 1 :])
    return jnp.moveaxis(x.reshape(*before, peers, -1, *after), dim, 0)


def sent_and_summed(x, axis, dim):
    peers = lax.axis_size(axis)
    blocks = lax.all_to_all(in_blocks(x, dim, peers), axis, 0, 0, tiled=True)
    return jnp.sum(blocks.astype(jnp.float32), axis=0)


def side_by_side(arrays, axis, dim, along):
    both = jnp.concatenate(arrays, axis=along)
    whole, at, done = (lax.all_gather(both, axis, axis=dim, tiled=True), 0, [])
    for a in arrays:
        done.append(lax.slice_in_dim(whole, at, at + a.shape[along], axis=along))
        at += a.shape[along]
    return tuple(done)


def newton_root(block):
    order = block.shape[0]
    vector = jnp.full((order,), 1.0 / math.sqrt(order), jnp.float32)
    length = jnp.ones((), jnp.float32)
    for turn_index in range(POWER):
        image = jnp.dot(block, vector.astype(jnp.bfloat16), preferred_element_type=jnp.float32)
        length = jnp.sqrt(jnp.sum(image * image))
        vector = image / length
    scaling = 2.5 / length
    identity = (
        lax.broadcasted_iota(jnp.int32, (order, order), 0)
        == lax.broadcasted_iota(jnp.int32, (order, order), 1)
    ).astype(jnp.float32)
    moment = scaling * block.astype(jnp.float32)
    moment_low = moment.astype(jnp.bfloat16)
    iterate = identity
    for turn_index in range(ITERS):
        factor = ((5.0 * identity - moment) * 0.25).astype(jnp.bfloat16)
        if turn_index == 0:
            iterate = factor.astype(jnp.float32)
        else:
            iterate = jnp.dot(
                iterate.astype(jnp.bfloat16), factor, preferred_element_type=jnp.float32
            )
        if turn_index + 1 < ITERS:
            square = jnp.dot(factor, factor, preferred_element_type=jnp.float32).astype(
                jnp.bfloat16
            )
            fourth = jnp.dot(square, square, preferred_element_type=jnp.float32).astype(
                jnp.bfloat16
            )
            moment = jnp.dot(fourth, moment_low, preferred_element_type=jnp.float32)
            moment_low = moment.astype(jnp.bfloat16)
    return (jnp.sqrt(jnp.sqrt(scaling)) * iterate).astype(jnp.bfloat16)


def body(tokens, cotangent, routing, stat_prev, root_prev, owner_map):
    expert_count = lax.axis_size("expert")
    group_count = lax.axis_size("group")
    my_expert = lax.axis_index("expert")
    my_group = lax.axis_index("group")
    tok_rows = tokens.shape[0]
    width_part = tokens.shape[1]
    hidden = cotangent.shape[1]
    row_block = stat_prev.shape[1]
    capacity = 2 * tok_rows // expert_count
    owners = expert_count // 4
    route = routing[:, 0]
    expert_ids = jnp.arange(expert_count, dtype=jnp.int32)
    onehot = (route[:, None] == expert_ids[None, :]).astype(jnp.int32)
    position = jnp.sum(onehot * (jnp.cumsum(onehot, axis=0) - 1), axis=1)
    column = route * capacity + position
    table = jnp.full((expert_count * capacity,), tok_rows, jnp.int32)
    table = table.at[column].set(jnp.arange(tok_rows, dtype=jnp.int32))
    tokens_pad = jnp.concatenate([tokens, jnp.zeros((1, width_part), tokens.dtype)], 0)
    signal_pad = jnp.concatenate([cotangent, jnp.zeros((1, hidden), cotangent.dtype)], 0)
    send_tokens = jnp.take(tokens_pad, table, axis=0).reshape(expert_count, capacity, width_part)
    send_signal = jnp.take(signal_pad, table, axis=0).reshape(expert_count, capacity, hidden)
    got_tokens, got_signal = in_one_piece((send_tokens, send_signal), "expert", 0, 0, 1)
    got_tokens = got_tokens.reshape(expert_count * capacity, width_part)
    got_signal = got_signal.reshape(expert_count * capacity, hidden)
    grad = lax.dot_general(
        got_tokens, got_signal, (((0,), (0,)), ((), ())), preferred_element_type=jnp.float32
    )
    grad = (grad * (1.0 / math.sqrt(tok_rows))).astype(jnp.bfloat16)
    gram_part = sent_and_summed(
        lax.dot_general(
            grad, grad, (((0,), (0,)), ((), ())), preferred_element_type=jnp.float32
        ).astype(jnp.bfloat16),
        "group",
        0,
    )
    stat_new = keep_share * stat_prev[0] + (1.0 - keep_share) * gram_part / (
        width_part * group_count
    )
    my_live = jnp.take(owner_map, my_expert) < owners
    stat_low = stat_new.astype(jnp.bfloat16)
    prev_rows = root_prev[0]
    stat_full, prev_full = side_by_side((stat_low, prev_rows), "group", 0, 1)
    root_full = lax.cond(my_live, lambda: newton_root(stat_full), lambda: prev_full)
    update = jnp.dot(grad, root_full, preferred_element_type=jnp.float32).astype(jnp.bfloat16)
    root_rows = lax.dynamic_slice_in_dim(root_full, my_group * row_block, row_block, 0)
    return (stat_new[None], root_rows[None], update[None])


def solution(mesh):
    in_specs = (
        P("expert", "group"),
        P("expert", None),
        P("expert", None),
        P("expert", "group", None),
        P("expert", "group", None),
        P(),
    )
    out_specs = (P("expert", "group", None), P("expert", "group", None), P("expert", "group", None))
    return jax.shard_map(body, mesh=mesh, in_specs=in_specs, out_specs=out_specs, check_vma=False)
```

profile of v0, /device:TPU:21, one launch (start us, length us, event | category | flops | bytes accessed | tf_op | source)
XLA Modules:
  0.0 353.8 jit_solution(6797006011569724644)
XLA Ops:
  7.2 0.0 copy-start.2
  7.2 0.0 all-gather.2.cloned.1.call-start
  7.2 0.8 iota_compare_fusion.1
  8.0 1.2 reduce-window.6
  9.2 0.2 slice_reduce_fusion
  9.5 0.1 bitcast_bitcast_fusion
  9.6 0.7 fusion.54
  10.3 0.7 compare_select_fusion
  11.0 2.9 scatter_custom_fusion
  14.0 1.3 concatenate.12
  15.3 0.0 copy-done.2
  15.3 0.1 concatenate.13
  15.3 5.3 %gather_fusion = bf16[960,1024]{1,0:T(8,128)(2,1)} fusion(bf16[481,1024]{1,0:T(8,128)(2,1)S(1)} %concatenate.12, s32[1024]{0:T(1024)S(1)} %pad_clamp_fusion), kind=kCustom, calls=%fused_computation.clone | custom fusion | bytes 3936000 | tf_op jit(solution)/shard_map/jit(_take)/gather | solution.py:98
  20.6 0.0 copy-start
  20.6 5.3 %gather_fusion.1 = bf16[960,1024]{1,0:T(8,128)(2,1)} fusion(bf16[481,1024]{1,0:T(8,128)(2,1)S(1)} %concatenate.13, s32[1024]{0:T(1024)S(1)} %pad_clamp_fusion), kind=kCustom, calls=%fused_computation.1.clone | custom fusion | bytes 3936000 | tf_op jit(solution)/shard_map/jit(_take)/gather | solution.py:99
  25.9 0.0 copy-done
  25.9 3.9 %broadcast_select_fusion.1 = (bf16[960,1024]{1,0:T(8,128)(2,1)}, bf16[960,1024]{1,0:T(8,128)(2,1)}) fusion(bf16[960,1024]{1,0:T(8,128)(2,1)S(1)} %copy-done, pred[960]{0:T(1024)(128)(4,1)S(1)} %compare_and_fusion, bf16[960,1024]{1,0:T(8,128)(2,1)} %gather_fusion.1), kind=kLoop, calls=%fused_computation.72 | loop fusion | flops 1966080 | bytes 7865280 | tf_op jit(solution)/shard_map/jit(_take)/select_n | solution.py:98
  29.8 2.6 reshape.48
  32.4 3.7 %reshape.49 = bf16[64,15,1024]{2,1,0:T(8,128)(2,1)} reshape(bf16[960,1024]{1,0:T(8,128)(2,1)} %get-tuple-element.26) | data formatting | bytes 3932160 | tf_op jit(solution)/shard_map/reshape | solution.py:99
  36.1 3.1 pad_maximum_fusion
  39.3 110.3 %all_to_all.10 = bf16[64,30,1024]{2,1,0:T(8,128)(2,1)S(1)} all-to-all(bf16[64,30,1024]{2,1,0:T(8,128)(2,1)S(1)} %pad_maximum_fusion), channel_id=1, replica_groups=mesh['expert'=64,'group'=4] {'expert'}, dimensions={0} | all-to-all | bytes 7864320 | tf_op jit(solution)/shard_map/all_to_all | solution.py:18
  149.5 1.5 fusion.57
  151.0 5.4 %fusion.49 = bf16[1024,1024]{1,0:T(8,128)(2,1)S(1)} fusion(bf16[64,15,1024]{2,1,0:T(8,128)(2,1)S(1)} %get-tuple-element.24, bf16[64,15,1024]{2,1,0:T(8,128)(2,1)S(1)} %get-tuple-element.23), kind=kOutput, calls=%fused_computation.66 | convolution fusion | flops 2015363072 | bytes 6029312 | tf_op jit(solution)/shard_map/dot_general | solution.py:103
  156.4 0.0 copy-start.5
  156.4 2.4 convolution_convert_fusion
  158.8 0.0 copy-done.5
  158.8 50.0 %all_to_all.11 = bf16[4,256,1024]{2,1,0:T(8,128)(2,1)S(1)} all-to-all(bf16[4,256,1024]{2,1,0:T(8,128)(2,1)S(1)} %bitcast.55), channel_id=1, replica_groups=mesh['expert'=64,'group'=4] {'group'}, dimensions={0} | all-to-all | bytes 4194304 | tf_op jit(solution)/shard_map/all_to_all | solution.py:29
  208.9 0.0 copy-start.1
  208.9 0.4 convert_reduce_fusion
  209.3 0.8 copy-done.1
  210.1 0.0 copy-start.3
  210.1 0.2 fusion.52
  210.3 0.0 copy-start.4
  210.3 0.8 copy-done.3
  211.1 1.1 pad_maximum_fusion.1
  212.2 0.0 all-gather.2.cloned.1.call-update
  212.2 0.0 copy-done.4
  212.2 0.6 dynamic-slice.2
  213.5 1.2 bitcast_add_fusion.1
  214.7 79.7 %all-gather.2.cloned.1.call-done = bf16[1024,2048]{1,0:T(8,128)(2,1)} async-done(((bf16[256,2048]{1,0:T(8,128)(2,1)}), bf16[1024,2048]{1,0:T(8,128)(2,1)}) %all-gather.2.cloned.1.call-update) | async-done | bytes 4194320 | tf_op jit(solution)/shard_map/all_gather | solution.py:35
  294.3 46.5 %conditional.1 = (bf16[1024,1024]{1,0:T(8,128)(2,1)S(1)}) conditional(s32[]{:T(128)} %bitcast.16, bf16[1024,2048]{1,0:T(8,128)(2,1)} %all-gather.2.cloned.1.call-done, bf16[1024,2048]{1,0:T(8,128)(2,1)} %all-gather.2.cloned.1.call-done), branch_computations={%region_5.7_spmd, %region_6.16_spmd} | conditional | flops 8632956928 | bytes 39997616 | solution.py:121
  294.3 2.2 fusion.22
  296.5 0.6 multiply_reduce_fusion.7
  297.9 2.2 fusion.46
  300.1 0.6 multiply_reduce_fusion.6
  301.4 2.2 fusion.44
  303.7 0.6 multiply_reduce_fusion.5
  305.0 2.2 fusion.42
  307.3 0.6 multiply_reduce_fusion.4
  308.6 2.2 fusion.40
  310.8 0.6 multiply_reduce_fusion.3
  312.2 2.2 fusion.38
  314.4 0.6 multiply_reduce_fusion.2
  315.7 2.2 fusion.36
  318.0 0.6 multiply_reduce_fusion.1
  319.3 2.2 fusion.34
  321.5 0.6 multiply_reduce_fusion
  322.9 4.6 %fusion.20 = bf16[1024,1024]{1,0:T(8,128)(2,1)S(1)} fusion(f32[]{:T(128)S(6)} %div.49, bf16[1024,2048]{1,0:T(8,128)(2,1)} %param.3), kind=kOutput, calls=%fused_computation.21 | convolution fusion | flops 2154823680 | bytes 4194308 | tf_op jit(solution)/shard_map/cond/branch_1_fun/dot_general | solution.py:67
  327.6 8.1 %fusion.5 = f32[1024,1024]{1,0:T(8,128)} fusion(f32[]{:T(128)S(6)} %div.49, bf16[1024,1024]{1,0:T(8,128)(2,1)S(1)} %fusion.20, bf16[1024,2048]{1,0:T(8,128)(2,1)} %param.3), kind=kOutput, calls=%fused_computation.13 | convolution fusion | flops 4299161600 | bytes 10485764 | tf_op jit(solution)/shard_map/cond/branch_1_fun/dot_general | solution.py:73
  335.6 5.2 %multiply_convert_fusion = bf16[1024,1024]{1,0:T(8,128)(2,1)S(1)} fusion(f32[1024,1024]{1,0:T(8,128)} %fusion.5, f32[]{:T(128)S(6)} %sqrt.29, f32[]{:T(128)S(6)} %div.49, bf16[1024,2048]{1,0:T(8,128)(2,1)} %param.3), kind=kOutput, calls=%fused_computation.9 | convolution fusion | flops 2162163712 | bytes 8388616 | tf_op jit(solution)/shard_map/cond/branch_1_fun/dot_general | solution.py:63
  340.8 5.2 %convert_bitcast_fusion = bf16[1,1024,1024]{2,1,0:T(8,128)(2,1)} fusion(bf16[1024,1024]{1,0:T(8,128)(2,1)} %copy-done.5, bf16[1024,1024]{1,0:T(8,128)(2,1)S(1)} %get-tuple-element.27), kind=kOutput, calls=%fused_computation.68 | convolution fusion | flops 2148532224 | bytes 6291456 | tf_op jit(solution)/shard_map/dot_general | solution.py:122
  346.1 0.8 dynamic-slice_bitcast_fusion
  (21 shorter events, 0.1 us)
Async XLA Ops:
  7.2 8.1 %copy-start.2 = (bf16[480,1024]{1,0:T(8,128)(2,1)S(1)}, bf16[480,1024]{1,0:T(8,128)(2,1)}, u32[]{:S(2)}) copy-start(bf16[480,1024]{1,0:T(8,128)(2,1)} %param.11) | copy-start | bytes 2949124
  7.2 287.1 %all-gather.2.cloned.1.call-start = ((), (), s32[]{:S(2)}) async-start(), calls=%async_computation.2 | async-start | bytes 5242880 | tf_op jit(solution)/shard_map/all_gather | solution.py:35
  20.6 5.3 %copy-start = (bf16[960,1024]{1,0:T(8,128)(2,1)S(1)}, bf16[960,1024]{1,0:T(8,128)(2,1)}, u32[]{:S(2)}) copy-start(bf16[960,1024]{1,0:T(8,128)(2,1)} %gather_fusion) | copy-start | bytes 5898244
  156.4 2.4 copy-start.5
  208.9 1.2 copy-start.1
  210.1 1.0 copy-start.3
  210.3 1.9 copy-start.4
Sparse Core Ops, SparseCore 0:
  212.3 81.9 all-gather.1
where the time goes:
time: 355 us; the launch traced here: 354 us
  blocking collectives  160 us (45%)
  waiting for transfers between devices  79.7 us (22%)
  matrix products  48.8 us (14%)
  local copies, waits for them, and re-layouts  26 us (7%)
  other arithmetic  18.4 us (5%)
  between operations  14.9 us (4%)
  loops' own time  5.74 us (2%)
    all_to_all x1, blocking collectives, in_one_piece(): lax.all_to_all(both, axis, split_axis=split_dim, concat_axis=concat_dim,...  110 us
    all_gather x1, waiting for transfers between devices, side_by_side(): whole, at, done = (lax.all_gather(both, axis, axis=dim, tiled=True), 0, [])  79.7 us
    all_to_all x1, blocking collectives, sent_and_summed(): blocks = lax.all_to_all(in_blocks(x, dim, peers), axis, 0, 0, tiled=True)  50 us
    dot_general x8, matrix products, newton_root(): jnp.dot(block, vector.astype(jnp.bfloat16), preferred_element_type=jnp.fl...  17.9 us
    dot_general x1, matrix products, newton_root(): moment = jnp.dot(fourth, moment_low, preferred_element_type=jnp.float32)  8.06 us
  transfers between devices with their start and end apart: 1, of which 1 were waited for; matrix products, arithmetic and copies ran while one was open for 0% of the time, Pallas kernels for 0%

commit v1 on v0

v1 whole, which is shorter than its diff:
```python
import functools
import math

import jax
import jax.numpy as jnp
from jax import lax
from jax.experimental import pallas as pl
from jax.experimental.pallas import tpu as pltpu
from jax.sharding import PartitionSpec as P

POWER = 8
KEEP = 0.9
SLOTS = 16
B = 128
PIECE = 9
MIB = 1024 * 1024


def vmem():
    return pl.BlockSpec(memory_space=pltpu.VMEM)


def smem():
    return pl.BlockSpec(memory_space=pltpu.SMEM)


def params(mib):
    return pltpu.CompilerParams(vmem_limit_bytes=mib * MIB)


def cost(flops, nbytes):
    return pl.CostEstimate(flops=int(flops), bytes_accessed=int(nbytes), transcendentals=0)


def outer(a, b):
    return lax.dot_general(a, b, (((0,), (0,)), ((), ())), preferred_element_type=jnp.float32)


def dot(a, b):
    return jnp.dot(a, b, preferred_element_type=jnp.float32)


def ones_where(mask):
    return jnp.where(mask, 1.0, 0.0).astype(jnp.bfloat16)


def dispatch_kernel(experts, rows, route_ref, tok_ref, sig_ref, out_ref, slot_ref):
    tokens = route_ref.shape[1]
    wide = tok_ref.shape[1]

    @pl.when(pl.program_id(0) == 0)
    def _():
        route = route_ref[...]
        hot = lax.broadcasted_iota(jnp.int32, (experts, tokens), 0) == route
        before = lax.broadcasted_iota(jnp.int32, (tokens, tokens), 0) < lax.broadcasted_iota(
            jnp.int32, (tokens, tokens), 1
        )
        earlier = dot(ones_where(hot), ones_where(before))
        position = jnp.sum(jnp.where(hot, earlier, 0.0), axis=0, keepdims=True)
        slot_ref[...] = route * SLOTS + position.astype(jnp.int32)

    at = lax.broadcasted_iota(jnp.int32, (rows, tokens), 0) + pl.program_id(0) * rows
    pick = ones_where(at == slot_ref[...])
    out_ref[:, :wide] = dot(pick, tok_ref[...]).astype(jnp.bfloat16)
    out_ref[:, wide:] = dot(pick, sig_ref[...]).astype(jnp.bfloat16)


def dispatch(route, tokens, signal, experts):
    count, wide = tokens.shape
    hidden = signal.shape[1]
    total, rows = experts * SLOTS, 256
    return pl.pallas_call(
        functools.partial(dispatch_kernel, experts, rows),
        grid=(total // rows,),
        in_specs=[
            pl.BlockSpec((1, count), lambda i: (0, 0)),
            pl.BlockSpec((count, wide), lambda i: (0, 0)),
            pl.BlockSpec((count, hidden), lambda i: (0, 0)),
        ],
        out_specs=pl.BlockSpec((rows, wide + hidden), lambda i: (i, 0)),
        out_shape=jax.ShapeDtypeStruct((total, wide + hidden), jnp.bfloat16),
        scratch_shapes=[pltpu.VMEM((1, count), jnp.int32)],
        compiler_params=params(24),
        cost_estimate=cost(2 * total * count * (wide + hidden), 6 * MIB),
        name="dispatch",
    )(route, tokens, signal)


def owned_blocks(d, group):
    found = [(d, d, 0, 0), (d, d, 0, 1), (d, d, 1, 1)]
    for h in range(group):
        if h > d:
            found += [(d, h, 0, 0), (d, h, 0, 1)]
        if h < d:
            found += [(h, d, 1, 0), (h, d, 1, 1)]
    return found


def gradient_kernel(group, scale, x_ref, grad_ref, part_ref):
    wide = grad_ref.shape[0]
    step = 2 * B
    for r in range(wide // step):
        block = outer(x_ref[:, r * step : (r + 1) * step], x_ref[:, wide:])
        grad_ref[r * step : (r + 1) * step, :] = (block * scale).astype(jnp.bfloat16)
    place = {}
    for d in range(group):
        for k, name in enumerate(owned_blocks(d, group)):
            place[name] = (d, k)
    for p in range(group):
        for q in range(p, group):
            gram = outer(
                grad_ref[:, p * step : (p + 1) * step], grad_ref[:, q * step : (q + 1) * step]
            ).astype(jnp.bfloat16)
            for i in range(2):
                for j in range(2):
                    if (p, q, i, j) in place:
                        d, k = place[(p, q, i, j)]
                        part_ref[d, k * B : (k + 1) * B, :] = gram[
                            i * B : (i + 1) * B, j * B : (j + 1) * B
                        ]


def gradient(x, group, wide, scale):
    total, both = x.shape
    hidden = both - wide
    return pl.pallas_call(
        functools.partial(gradient_kernel, group, scale),
        in_specs=[vmem()],
        out_specs=(vmem(), vmem()),
        out_shape=(
            jax.ShapeDtypeStruct((wide, hidden), jnp.bfloat16),
            jax.ShapeDtypeStruct((group, PIECE * B, B), jnp.bfloat16),
        ),
        compiler_params=params(32),
        cost_estimate=cost(2 * wide * hidden * (total + hidden), 8 * MIB),
        name="gradient",
    )(x)


def statistic_kernel(group, full, me_ref, parts_ref, prev_ref, stat_ref, own_ref):
    me = me_ref[0]

    def gram(k):
        total = parts_ref[0, k * B : (k + 1) * B, :].astype(jnp.float32)
        for s in range(1, group):
            total += parts_ref[s, k * B : (k + 1) * B, :].astype(jnp.float32)
        return total

    def put(k, block, row, col):
        at = (slice(row, row + B), pl.ds(pl.multiple_of(col, B), B))
        new = KEEP * prev_ref[at] + (1.0 - KEEP) * block / full
        stat_ref[at] = new
        own_ref[k * B : (k + 1) * B, :] = new.astype(jnp.bfloat16)

    mine = me * 2 * B
    put(0, gram(0), 0, mine)
    put(1, gram(1), 0, mine + B)
    put(2, gram(2), B, mine + B)
    for j in range(group - 1):
        k = 3 + 2 * j

        @pl.when(j >= me)
        def _():
            col = (j + 1) * 2 * B
            put(k, gram(k), 0, col)
            put(k + 1, gram(k + 1), 0, col + B)

        @pl.when(j < me)
        def _():
            col = j * 2 * B + B
            put(k, gram(k).T, 0, col)
            put(k + 1, gram(k + 1).T, B, col)


def new_statistic(me, parts, prev, full):
    group = parts.shape[0]
    return pl.pallas_call(
        functools.partial(statistic_kernel, group, float(full)),
        in_specs=[smem(), vmem(), vmem()],
        out_specs=(vmem(), vmem()),
        out_shape=(
            jax.ShapeDtypeStruct(prev.shape, jnp.float32),
            jax.ShapeDtypeStruct((PIECE * B, B), jnp.bfloat16),
        ),
        compiler_params=params(16),
        cost_estimate=cost(4 * prev.size, 4 * MIB),
        name="statistic",
    )(me, parts, prev)


def root_kernel(group, flags_ref, pieces_ref, part_ref, stat_ref, root_ref, a_ref, f_ref, g_ref, h_ref):
    me, live = flags_ref[0], flags_ref[1]
    order = a_ref.shape[0]
    step = 2 * B

    def fill(block, row, col, mirror=True):
        a_ref[row : row + B, col : col + B] = block
        if mirror:
            a_ref[col : col + B, row : row + B] = block.T

    for s in range(group):
        at = s * step
        block = [pieces_ref[s, k * B : (k + 1) * B, :] for k in range(PIECE)]
        fill(block[0], at, at, False)
        fill(block[1], at, at + B)
        fill(block[2], at + B, at + B, False)
        k = 3
        for h in range(group):
            if h > s:
                fill(block[k], at, h * step)
                fill(block[k + 1], at, h * step + B)
            if h < s:
                fill(block[k], at, h * step + B)
                fill(block[k + 1], at + B, h * step + B)
            if h != s:
                k += 2

    row = lax.broadcasted_iota(jnp.int32, (step, step), 0)
    col = lax.broadcasted_iota(jnp.int32, (step, step), 1)
    mine = pl.multiple_of(me * step, step)
    for h in range(group):
        own = (row < jnp.where(h < me, 0, B)) | (col >= jnp.where(h > me, step, B))
        low = a_ref[pl.ds(mine, step), h * step : (h + 1) * step].astype(jnp.float32)
        at = (slice(None), slice(h * step, (h + 1) * step))
        stat_ref[at] = jnp.where(own, part_ref[at], low)

    @pl.when(live != 0)
    def _():
        def power(_, carry):
            vector, _ = carry
            image = dot(vector.astype(jnp.bfloat16), a_ref[...])
            length = jnp.sqrt(jnp.sum(image * image, axis=1, keepdims=True))
            return image / length, length

        vector = jnp.full((16, order), 1.0 / math.sqrt(order), jnp.float32)
        length = jnp.ones((16, 1), jnp.float32)
        _, length = lax.fori_loop(0, POWER, power, (vector, length))
        scaling = 2.5 / length[:1, :1]
        quarter = jnp.sqrt(jnp.sqrt(scaling)) * 0.25

        def rows_of(i):
            return pl.ds(pl.multiple_of(i * step, step), step)

        def first(i, _):
            here = rows_of(i)
            line = lax.broadcasted_iota(jnp.int32, (step, order), 0) + i * step
            eye = line == lax.broadcasted_iota(jnp.int32, (step, order), 1)
            moment = scaling * a_ref[here, :].astype(jnp.float32)
            f_ref[here, :] = ((jnp.where(eye, 5.0, 0.0) - moment) * 0.25).astype(jnp.bfloat16)
            return 0

        lax.fori_loop(0, order // step, first, 0)

        def second(i, _):
            here = rows_of(i)
            factor = f_ref[here, :]
            square = dot(factor, f_ref[...])
            g_ref[here, :] = square.astype(jnp.bfloat16)
            h_ref[here, :] = (5.0 * factor.astype(jnp.float32) - 4.0 * square).astype(jnp.bfloat16)
            return 0

        lax.fori_loop(0, order // step, second, 0)

        def third(i, _):
            here = rows_of(i)
            a_ref[here, :] = dot(g_ref[here, :], g_ref[...]).astype(jnp.bfloat16)
            return 0

        lax.fori_loop(0, order // step, third, 0)

        def last(i, _):
            here = rows_of(i)
            tail = dot(a_ref[here, :], h_ref[...])
            factor = f_ref[here, :].astype(jnp.float32)
            root_ref[here, :] = ((5.0 * factor - tail) * quarter).astype(jnp.bfloat16)
            return 0

        lax.fori_loop(0, order // step, last, 0)


def inverse_root(flags, pieces, part, order):
    group = pieces.shape[0]
    square = pltpu.VMEM((order, order), jnp.bfloat16)
    return pl.pallas_call(
        functools.partial(root_kernel, group),
        in_specs=[smem(), vmem(), vmem()],
        out_specs=(vmem(), vmem()),
        out_shape=(
            jax.ShapeDtypeStruct(part.shape, jnp.float32),
            jax.ShapeDtypeStruct((order, order), jnp.bfloat16),
        ),
        scratch_shapes=[square] * 4,
        compiler_params=params(32),
        cost_estimate=cost(6 * order**3, 8 * MIB),
        name="root",
    )(flags, pieces, part)


def update_kernel(group, flags_ref, grad_ref, root_ref, *refs):
    prev_refs, (update_ref, rows_ref, whole_ref) = refs[:group], refs[group:]
    me, live = flags_ref[0], flags_ref[1]
    step = prev_refs[0].shape[0]

    def rows_of(i):
        return pl.ds(pl.multiple_of(i * step, step), step)

    @pl.when(live != 0)
    def _():
        rows_ref[...] = root_ref[rows_of(me), :]

        def line(i, _):
            here = rows_of(i)
            update_ref[here, :] = dot(grad_ref[here, :], root_ref[...]).astype(jnp.bfloat16)
            return 0

        lax.fori_loop(0, grad_ref.shape[0] // step, line, 0)

    @pl.when(live == 0)
    def _():
        rows_ref[...] = prev_refs[0][...]
        for k in range(group):
            source = lax.rem(me - k + group, group)
            whole_ref[rows_of(source), :] = prev_refs[k][...]

        def line(i, _):
            here = rows_of(i)
            update_ref[here, :] = dot(grad_ref[here, :], whole_ref[...]).astype(jnp.bfloat16)
            return 0

        lax.fori_loop(0, grad_ref.shape[0] // step, line, 0)


def updated(flags, grad, root, prevs):
    group = len(prevs)
    wide, order = grad.shape
    return pl.pallas_call(
        functools.partial(update_kernel, group),
        in_specs=[smem()] + [vmem()] * (2 + group),
        out_specs=(vmem(), vmem()),
        out_shape=(
            jax.ShapeDtypeStruct((wide, order), jnp.bfloat16),
            jax.ShapeDtypeStruct(prevs[0].shape, jnp.bfloat16),
        ),
        scratch_shapes=[pltpu.VMEM((order, order), jnp.bfloat16)],
        compiler_params=params(32),
        cost_estimate=cost(2 * wide * order * order, 8 * MIB),
        name="update",
    )(flags, grad, root, *prevs)


def body(tokens, cotangent, routing, stat_prev, root_prev, owner_map):
    experts = lax.axis_size("expert")
    group = lax.axis_size("group")
    my_expert = lax.axis_index("expert")
    me = lax.axis_index("group").astype(jnp.int32)
    rows, wide = tokens.shape
    order = cotangent.shape[1]
    owners = experts // 4
    live = (jnp.take(owner_map, my_expert) < owners).astype(jnp.int32)
    flags = jnp.stack([me, live])

    sent = dispatch(routing.reshape(1, rows), tokens, cotangent, experts)
    sent = sent.reshape(experts, SLOTS, wide + order)
    got = lax.all_to_all(sent, "expert", 0, 0, tiled=True)
    got = got.reshape(experts * SLOTS, wide + order)
    grad, part = gradient(got, group, wide, 1.0 / math.sqrt(rows))
    parts = lax.all_to_all(part, "group", 0, 0, tiled=True)
    stat_own, own = new_statistic(flags, parts, stat_prev[0], wide * group)
    copies = jnp.broadcast_to(own[None], (group,) + own.shape)
    pieces = lax.all_to_all(copies, "group", 0, 0, tiled=True)
    prev, pieces = lax.optimization_barrier((root_prev[0], pieces))
    prevs = [prev]
    for k in range(1, group):
        ring = [(g, (g + k) % group) for g in range(group)]
        prevs.append(lax.ppermute(prev, "group", ring))
    stat, root = inverse_root(flags, pieces, stat_own, order)
    update, root_rows = updated(flags, grad, root, prevs)
    return stat[None], root_rows[None], update[None]


def solution(mesh):
    in_specs = (
        P("expert", "group"),
        P("expert", None),
        P("expert", None),
        P("expert", "group", None),
        P("expert", "group", None),
        P(),
    )
    out_specs = (P("expert", "group", None), P("expert", "group", None), P("expert", "group", None))
    return jax.shard_map(body, mesh=mesh, in_specs=in_specs, out_specs=out_specs, check_vma=False)
```

time: 355 us -> 244 us (0.69)
  the two profiles are of different devices: /device:TPU:21 before, /device:TPU:32 now
where the time goes in v1:
time: 244 us; the launch traced here: 243 us
  blocking collectives  146 us (60%)
  waiting for transfers between devices  66.7 us (27%)
  Pallas kernels  16.1 us (7%)
  starting transfers between devices  8.05 us (3%)
  local copies, waits for them, and re-layouts  5.15 us (2%)
    all_to_all x1, blocking collectives, body(): got = lax.all_to_all(sent, 'expert', 0, 0, tiled=True)  113 us
    ppermute x3, waiting for transfers between devices, body(): prevs.append(lax.ppermute(prev, 'group', ring))  41.7 us
    all_to_all x1, blocking collectives, body(): pieces = lax.all_to_all(copies, 'group', 0, 0, tiled=True)  33 us
    all_to_all x1, waiting for transfers between devices, body(): parts = lax.all_to_all(part, 'group', 0, 0, tiled=True)  25 us
    pallas_call x1, Pallas kernels, updated(): pl.pallas_call(functools.partial(update_kernel, group), in_specs=[smem()]...  5.06 us
    pallas_call x1, Pallas kernels, gradient(): pl.pallas_call(functools.partial(gradient_kernel, group, scale), in_specs...  5.01 us
  transfers between devices with their start and end apart: 4, of which 4 were waited for; matrix products, arithmetic and copies ran while one was open for 0% of the time, Pallas kernels for 1%

profile of v1, /device:TPU:32, one launch (start us, length us, event | category | flops | bytes accessed | tf_op | source)
XLA Modules:
  0.0 243.3 jit_solution(8986636685226350084)
XLA Ops:
  0.6 0.0 copy-start.1
  0.6 1.2 copy-done.1
  1.8 0.0 copy-start.2
  1.8 1.2 copy-done.2
  3.0 0.0 copy-start.4
  3.0 0.7 copy-done.4
  3.7 3.1 %dispatch.1 = bf16[1024,2048]{1,0:T(8,128)(2,1)S(1)} custom-call(s32[1,480]{1,0:T(1,128)S(1)} %bitcast.17, bf16[480,1024]{1,0:T(8,128)(2,1)S(1)} %copy-done.1, bf16[480,1024]{1,0:T(8,128)(2,1)S(1)} %copy-done.2), custom_call_target="tpu_custom_call" | custom-call | flops 2013265920 | bytes 6291456 | tf_op jit(solution)/shard_map/dispatch/pallas_call | solution.py:72
  6.8 112.9 %all_to_all.15 = bf16[64,16,2048]{2,1,0:T(8,128)(2,1)S(1)} all-to-all(bf16[64,16,2048]{2,1,0:T(8,128)(2,1)S(1)} %bitcast.11), channel_id=1, replica_groups=mesh['expert'=64,'group'=4] {'expert'}, dimensions={0} | all-to-all | bytes 8388608 | tf_op jit(solution)/shard_map/all_to_all | solution.py:364
  119.7 5.0 %gradient.1 = (bf16[1024,1024]{1,0:T(8,128)(2,1)S(1)}, bf16[4,1152,128]{2,1,0:T(8,128)(2,1)}) custom-call(bf16[1024,2048]{1,0:T(8,128)(2,1)S(1)} %bitcast.10), custom_call_target="tpu_custom_call" | custom-call | flops 4294967296 | bytes 8388608 | tf_op jit(solution)/shard_map/gradient/pallas_call | solution.py:126
  124.7 0.0 copy-start.5
  124.7 1.3 copy-done.5
  126.0 0.0 copy-start.7
  126.0 0.0 copy-start
  126.0 3.9 %all-to-all-start.1 = ((bf16[4,1152,128]{2,1,0:T(8,128)(2,1)}), bf16[4,1152,128]{2,1,0:T(8,128)(2,1)S(1)}, u32[]{:S(2)}, u32[]{:S(2)}) async-start(bf16[4,1152,128]{2,1,0:T(8,128)(2,1)} %get-tuple-element.13), calls=%async_computation.1 | async-start | bytes 2359296 | tf_op jit(solution)/shard_map/all_to_all | solution.py:367
  129.9 0.0 copy-done.7
  129.9 0.6 dynamic-slice.2
  131.2 0.1 pad_add_fusion.me_ref.flags_ref
  131.2 25.0 %all-to-all-done.1.parts_ref = bf16[4,1152,128]{2,1,0:T(8,128)(2,1)S(1)} async-done(((bf16[4,1152,128]{2,1,0:T(8,128)(2,1)}), bf16[4,1152,128]{2,1,0:T(8,128)(2,1)S(1)}, u32[]{:S(2)}, u32[]{:S(2)}) %all-to-all-start.1) | async-done | bytes 1179680 | tf_op jit(solution)/shard_map/all_to_all | solution.py:367
  156.3 0.0 copy-done
  156.3 0.8 statistic.1
  157.1 0.0 copy-start.3
  157.1 0.2 broadcast_in_dim.20
  157.3 33.0 %all_to_all.16.pieces_ref = bf16[4,1152,128]{2,1,0:T(8,128)(2,1)S(1)} all-to-all(bf16[4,1152,128]{2,1,0:T(8,128)(2,1)S(1)} %broadcast_in_dim.20), channel_id=1, replica_groups=mesh['expert'=64,'group'=4] {'group'}, dimensions={0} | all-to-all | bytes 2359296 | tf_op jit(solution)/shard_map/all_to_all | solution.py:370
  190.3 0.0 copy-done.3
  190.3 0.6 collective-permute-start
  190.8 3.6 %collective-permute-start.1 = (bf16[256,1024]{1,0:T(8,128)(2,1)S(1)}, bf16[256,1024]{1,0:T(8,128)(2,1)S(1)}, u32[]{:S(2)}, u32[]{:S(2)}) collective-permute-start(bf16[256,1024]{1,0:T(8,128)(2,1)S(1)} %bitcast.14), channel_id=1, source_target_pairs={{0,2},{1,3},{2,0},{3,1},{4,6},{5,7},{6,4},{7,5},{8,10},{9,11},{10,... | collective-permute-start | bytes 1572872 | tf_op jit(solution)/shard_map/ppermute | solution.py:375
  194.4 0.0 collective-permute-start.2
  194.4 0.0 copy-start.6
  194.4 2.1 root.1
  196.5 28.9 %collective-permute-done.refs_1_ = bf16[256,1024]{1,0:T(8,128)(2,1)S(1)} collective-permute-done((bf16[256,1024]{1,0:T(8,128)(2,1)S(1)}, bf16[256,1024]{1,0:T(8,128)(2,1)S(1)}, u32[]{:S(2)}, u32[]{:S(2)}) %collective-permute-start) | collective-permute-done | bytes 524320 | tf_op jit(solution)/shard_map/ppermute | solution.py:375
  225.5 9.5 %collective-permute-done.1.refs_2_ = bf16[256,1024]{1,0:T(8,128)(2,1)S(1)} collective-permute-done((bf16[256,1024]{1,0:T(8,128)(2,1)S(1)}, bf16[256,1024]{1,0:T(8,128)(2,1)S(1)}, u32[]{:S(2)}, u32[]{:S(2)}) %collective-permute-start.1) | collective-permute-done | bytes 524320 | tf_op jit(solution)/shard_map/ppermute | solution.py:375
  235.0 3.2 %collective-permute-done.2.refs_3_ = bf16[256,1024]{1,0:T(8,128)(2,1)S(1)} collective-permute-done((bf16[256,1024]{1,0:T(8,128)(2,1)S(1)}, bf16[256,1024]{1,0:T(8,128)(2,1)S(1)}, u32[]{:S(2)}, u32[]{:S(2)}) %collective-permute-start.2) | collective-permute-done | bytes 524320 | tf_op jit(solution)/shard_map/ppermute | solution.py:375
  238.2 0.0 copy-done.6
  238.2 5.1 %update.1 = (bf16[1024,1024]{1,0:T(8,128)(2,1)}, bf16[256,1024]{1,0:T(8,128)(2,1)}) custom-call(s32[2]{0:T(128)S(1)} %pad_add_fusion.me_ref.flags_ref, bf16[1024,1024]{1,0:T(8,128)(2,1)S(1)} %copy-done.6, bf16[1024,1024]{1,0:T(8,128)(2,1)S(1)} %get-tuple-element.19.root_ref, bf16[256,1024]{1,0:T(8,128)(2,1)S(1)} %bitcast.16, ...), custom_call_target="tpu_custom_call" | custom-call | flops 2147483648 | bytes 8388608 | tf_op jit(solution)/shard_map/update/pallas_call | solution.py:336
Async XLA Ops:
  0.6 1.2 copy-start.1
  1.8 1.2 copy-start.2
  3.0 0.7 copy-start.4
  124.7 1.3 copy-start.5
  126.0 3.9 %copy-start.7 = (s32[64]{0:T(128)S(1)}, s32[64]{0:T(128)}, u32[]{:S(2)}) copy-start(s32[64]{0:T(128)} %param.11) | copy-start | bytes 772
  126.0 30.2 %copy-start = (f32[1,256,1024]{2,1,0:T(8,128)S(1)}, f32[1,256,1024]{2,1,0:T(8,128)}, u32[]{:S(2)}) copy-start(f32[1,256,1024]{2,1,0:T(8,128)} %param.9) | copy-start | bytes 3145732
  126.0 30.2 %all-to-all-start.1 = ((bf16[4,1152,128]{2,1,0:T(8,128)(2,1)}), bf16[4,1152,128]{2,1,0:T(8,128)(2,1)S(1)}, u32[]{:S(2)}, u32[]{:S(2)}) async-start(bf16[4,1152,128]{2,1,0:T(8,128)(2,1)} %get-tuple-element.13), calls=%async_computation.1 | async-start | bytes 2359296 | tf_op jit(solution)/shard_map/all_to_all | solution.py:367
  157.1 33.1 %copy-start.3 = (bf16[1,256,1024]{2,1,0:T(8,128)(2,1)S(1)}, bf16[1,256,1024]{2,1,0:T(8,128)(2,1)}, u32[]{:S(2)}) copy-start(bf16[1,256,1024]{2,1,0:T(8,128)(2,1)} %param.10) | copy-start | bytes 1572868
  190.3 35.2 %collective-permute-start = (bf16[256,1024]{1,0:T(8,128)(2,1)S(1)}, bf16[256,1024]{1,0:T(8,128)(2,1)S(1)}, u32[]{:S(2)}, u32[]{:S(2)}) collective-permute-start(bf16[256,1024]{1,0:T(8,128)(2,1)S(1)} %bitcast.13), channel_id=1, source_target_pairs={{0,1},{1,2},{2,3},{3,0},{4,5},{5,6},{6,7},{7,4},{8,9},{9,10},{10,1... | collective-permute-start | bytes 1572872 | tf_op jit(solution)/shard_map/ppermute | solution.py:375
  190.8 44.1 %collective-permute-start.1 = (bf16[256,1024]{1,0:T(8,128)(2,1)S(1)}, bf16[256,1024]{1,0:T(8,128)(2,1)S(1)}, u32[]{:S(2)}, u32[]{:S(2)}) collective-permute-start(bf16[256,1024]{1,0:T(8,128)(2,1)S(1)} %bitcast.14), channel_id=1, source_target_pairs={{0,2},{1,3},{2,0},{3,1},{4,6},{5,7},{6,4},{7,5},{8,10},{9,11},{10,... | collective-permute-start | bytes 1572872 | tf_op jit(solution)/shard_map/ppermute | solution.py:375
  194.4 43.8 %collective-permute-start.2 = (bf16[256,1024]{1,0:T(8,128)(2,1)S(1)}, bf16[256,1024]{1,0:T(8,128)(2,1)S(1)}, u32[]{:S(2)}, u32[]{:S(2)}) collective-permute-start(bf16[256,1024]{1,0:T(8,128)(2,1)S(1)} %bitcast.15), channel_id=1, source_target_pairs={{0,3},{1,0},{2,1},{3,2},{4,7},{5,4},{6,5},{7,6},{8,11},{9,8},{10,9... | collective-permute-start | bytes 1572872 | tf_op jit(solution)/shard_map/ppermute | solution.py:375
  194.4 43.8 %copy-start.6 = (bf16[1024,1024]{1,0:T(8,128)(2,1)S(1)}, bf16[1024,1024]{1,0:T(8,128)(2,1)}, u32[]{:S(2)}) copy-start(bf16[1024,1024]{1,0:T(8,128)(2,1)} %copy-done.5) | copy-start | bytes 6291460

commit v2 on v1

v2 whole, which is shorter than its diff:
```python
import functools
import math

import jax
import jax.numpy as jnp
from jax import lax
from jax.experimental import pallas as pl
from jax.experimental.pallas import tpu as pltpu
from jax.sharding import PartitionSpec as P

POWER = 8
KEEP = 0.9
SLOTS = 16
B = 128
HALF = 8
PIECE = 9
MIB = 1024 * 1024


def vmem():
    return pl.BlockSpec(memory_space=pltpu.VMEM)


def smem():
    return pl.BlockSpec(memory_space=pltpu.SMEM)


def params(mib):
    return pltpu.CompilerParams(vmem_limit_bytes=mib * MIB)


def cost(flops, nbytes):
    return pl.CostEstimate(flops=int(flops), bytes_accessed=int(nbytes), transcendentals=0)


def outer(a, b):
    return lax.dot_general(a, b, (((0,), (0,)), ((), ())), preferred_element_type=jnp.float32)


def dot(a, b):
    return jnp.dot(a, b, preferred_element_type=jnp.float32)


def ones_where(mask):
    return jnp.where(mask, 1.0, 0.0).astype(jnp.bfloat16)


def dispatch_kernel(experts, route_hbm, tok_hbm, sig_hbm, out_ref, route_ref, slot_ref, tok_ref, sig_ref, sems):
    tokens = route_ref.shape[1]
    wide = tok_ref.shape[1]
    rows = out_ref.shape[0]

    @pl.when(pl.program_id(0) == 0)
    def _():
        copies = [
            pltpu.make_async_copy(route_hbm, route_ref, sems.at[0]),
            pltpu.make_async_copy(tok_hbm, tok_ref, sems.at[1]),
            pltpu.make_async_copy(sig_hbm, sig_ref, sems.at[2]),
        ]
        for copy in copies:
            copy.start()
        before = lax.broadcasted_iota(jnp.int32, (tokens, tokens), 0) < lax.broadcasted_iota(
            jnp.int32, (tokens, tokens), 1
        )
        before = ones_where(before)
        copies[0].wait()
        route = route_ref[...]
        hot = lax.broadcasted_iota(jnp.int32, (experts, tokens), 0) == route
        earlier = dot(ones_where(hot), before)
        position = jnp.sum(jnp.where(hot, earlier, 0.0), axis=0, keepdims=True)
        slot_ref[...] = route * SLOTS + position.astype(jnp.int32)
        copies[1].wait()
        copies[2].wait()

    at = lax.broadcasted_iota(jnp.int32, (rows, tokens), 0) + pl.program_id(0) * rows
    pick = ones_where(at == slot_ref[...])
    out_ref[:, :wide] = dot(pick, tok_ref[...]).astype(jnp.bfloat16)
    out_ref[:, wide:] = dot(pick, sig_ref[...]).astype(jnp.bfloat16)


def dispatch(route, tokens, signal, experts):
    count, wide = tokens.shape
    hidden = signal.shape[1]
    total, rows = experts * SLOTS, 2 * B
    return pl.pallas_call(
        functools.partial(dispatch_kernel, experts),
        grid=(total // rows,),
        in_specs=[pl.BlockSpec(memory_space=pl.ANY)] * 3,
        out_specs=pl.BlockSpec((rows, wide + hidden), lambda i: (i, 0)),
        out_shape=jax.ShapeDtypeStruct((total, wide + hidden), jnp.bfloat16),
        scratch_shapes=[
            pltpu.VMEM((1, count), jnp.int32),
            pltpu.VMEM((1, count), jnp.int32),
            pltpu.VMEM((count, wide), jnp.bfloat16),
            pltpu.VMEM((count, hidden), jnp.bfloat16),
            pltpu.SemaphoreType.DMA((3,)),
        ],
        compiler_params=params(60),
        cost_estimate=cost(2 * total * count * (wide + hidden), 6 * MIB),
        name="dispatch",
    )(route, tokens, signal)


def owned_blocks(d, group):
    found = [(d, d, 0, 0), (d, d, 0, 1), (d, d, 1, 1)]
    for h in range(group):
        if h > d:
            found += [(d, h, 0, 0), (d, h, 0, 1)]
        if h < d:
            found += [(h, d, 1, 0), (h, d, 1, 1)]
    return found


def gradient_kernel(group, scale, x_hbm, grad_hbm, part_hbm, x_ref, grad_ref, part_ref, sems):
    wide = grad_ref.shape[0]
    step = 2 * B
    lines = wide // step
    loads = [pltpu.make_async_copy(x_hbm.at[:, wide:], x_ref.at[:, wide:], sems.at[0])]
    stores = []
    for r in range(lines):
        at = slice(r * step, (r + 1) * step)
        loads.append(pltpu.make_async_copy(x_hbm.at[:, at], x_ref.at[:, at], sems.at[1 + r]))
        stores.append(pltpu.make_async_copy(grad_ref.at[at, :], grad_hbm.at[at, :], sems.at[1 + lines + r]))
    for load in loads:
        load.start()
    loads[0].wait()
    for r in range(lines):
        loads[1 + r].wait()
        at = slice(r * step, (r + 1) * step)
        grad_ref[at, :] = (outer(x_ref[:, at], x_ref[:, wide:]) * scale).astype(jnp.bfloat16)
        stores[r].start()
    place = {}
    for d in range(group):
        for k, name in enumerate(owned_blocks(d, group)):
            place[name] = (d, k)
    last = {d: max((p, q) for (p, q, _, _) in owned_blocks(d, group)) for d in range(group)}
    for p in range(group):
        for q in range(p, group):
            gram = outer(
                grad_ref[:, p * step : (p + 1) * step], grad_ref[:, q * step : (q + 1) * step]
            ).astype(jnp.bfloat16)
            for i in range(2):
                for j in range(2):
                    if (p, q, i, j) in place:
                        d, k = place[(p, q, i, j)]
                        part_ref[d, k * B : (k + 1) * B, :] = gram[
                            i * B : (i + 1) * B, j * B : (j + 1) * B
                        ]
            for d in range(group):
                if last[d] == (p, q):
                    sem = sems.at[1 + 2 * lines + d]
                    stores.append(pltpu.make_async_copy(part_ref.at[d], part_hbm.at[d], sem))
                    stores[-1].start()
    for store in stores:
        store.wait()


def gradient(x, group, wide, scale):
    total, both = x.shape
    hidden = both - wide
    part = (group, PIECE * B, B)
    return pl.pallas_call(
        functools.partial(gradient_kernel, group, scale),
        in_specs=[pl.BlockSpec(memory_space=pl.ANY)],
        out_specs=(pl.BlockSpec(memory_space=pl.ANY),) * 2,
        out_shape=(
            jax.ShapeDtypeStruct((wide, hidden), jnp.bfloat16),
            jax.ShapeDtypeStruct(part, jnp.bfloat16),
        ),
        scratch_shapes=[
            pltpu.VMEM(x.shape, jnp.bfloat16),
            pltpu.VMEM((wide, hidden), jnp.bfloat16),
            pltpu.VMEM(part, jnp.bfloat16),
            pltpu.SemaphoreType.DMA((1 + 2 * (wide // (2 * B)) + group,)),
        ],
        compiler_params=params(60),
        cost_estimate=cost(2 * wide * hidden * (total + hidden), 10 * MIB),
        name="gradient",
    )(x)


def statistic_kernel(
    group, full, flags_ref, parts_ref, prev_ref, root_ref, stat_hbm, send_ref, stat_ref, own_ref, sem
):
    me, live = flags_ref[0], flags_ref[1]

    def gram(k):
        total = parts_ref[0, k * B : (k + 1) * B, :].astype(jnp.float32)
        for s in range(1, group):
            total += parts_ref[s, k * B : (k + 1) * B, :].astype(jnp.float32)
        return total

    def put(k, block, row, col):
        at = (slice(row, row + B), pl.ds(pl.multiple_of(col, B), B))
        new = KEEP * prev_ref[at] + (1.0 - KEEP) * block / full
        stat_ref[at] = new
        own_ref[k * B : (k + 1) * B, :] = new.astype(jnp.bfloat16)

    mine = pl.multiple_of(me * 2 * B, 2 * B)
    put(0, gram(0), 0, mine)
    put(1, gram(1), 0, mine + B)
    put(2, gram(2), B, mine + B)
    for j in range(group - 1):
        k = 3 + 2 * j

        @pl.when(j >= me)
        def _():
            col = (j + 1) * 2 * B
            put(k, gram(k), 0, col)
            put(k + 1, gram(k + 1), 0, col + B)

        @pl.when(j < me)
        def _():
            col = j * 2 * B + B
            put(k, gram(k).T, 0, col)
            put(k + 1, gram(k + 1).T, B, col)

    stat_ref[B:, pl.ds(mine, B)] = stat_ref[:B, pl.ds(mine + B, B)].T
    store = pltpu.make_async_copy(stat_ref, stat_hbm, sem)
    store.start()

    @pl.when(live != 0)
    def _():
        for t in range(group):
            send_ref[t, : PIECE * B, :] = own_ref[...]

    @pl.when(live == 0)
    def _():
        for t in range(group):
            for c in range(HALF):
                send_ref[t, (2 + c) * B : (3 + c) * B, :] = root_ref[B:, c * B : (c + 1) * B]
            send_ref[t, : 2 * B, :] = own_ref[pl.ds(shared(me, t), 2 * B), :]

    store.wait()


def shared(s, t):
    other = jnp.where(t > s, t - 1, jnp.minimum(t, PIECE // 2 - 2))
    return pl.multiple_of((3 + 2 * other) * B, B)


def new_statistic(flags, parts, prev, root, full):
    group = parts.shape[0]
    return pl.pallas_call(
        functools.partial(statistic_kernel, group, float(full)),
        in_specs=[smem(), vmem(), vmem(), vmem()],
        out_specs=(pl.BlockSpec(memory_space=pl.ANY), vmem()),
        out_shape=(
            jax.ShapeDtypeStruct(prev.shape, jnp.float32),
            jax.ShapeDtypeStruct((group, (2 + HALF) * B, B), jnp.bfloat16),
        ),
        scratch_shapes=[
            pltpu.VMEM(prev.shape, jnp.float32),
            pltpu.VMEM((PIECE * B, B), jnp.bfloat16),
            pltpu.SemaphoreType.DMA,
        ],
        compiler_params=params(8),
        cost_estimate=cost(4 * prev.size, 4 * MIB),
        name="statistic",
    )(flags, parts, prev, root)


def root_kernel(
    group,
    flags_ref,
    pieces_ref,
    prev_ref,
    grad_hbm,
    part_hbm,
    stat_hbm,
    rows_ref,
    update_hbm,
    a_ref,
    f_ref,
    g_ref,
    h_ref,
    grad_ref,
    mirror_ref,
    sems,
):
    me, live = flags_ref[0], flags_ref[1]
    order = a_ref.shape[0]
    step = 2 * B
    done = sems.at[2 * group - 2]
    load = pltpu.make_async_copy(grad_hbm, grad_ref, sems.at[2 * group - 1])

    @pl.when(live != 0)
    def _():
        load.start()

    def mirrored(j):
        s = jnp.where(j < me, j, j + 1)
        start = jnp.where(live != 0, shared(s, me), 0)
        col = pl.multiple_of(s * step, step)
        found = []
        for k in range(2):
            at = pl.ds(pl.multiple_of(start + k * B, B), B)
            mirror_ref[2 * j + k] = pieces_ref[s, at, :].astype(jnp.float32).T
            row = jnp.where(j < me, k * B, B)
            place = col + jnp.where(j < me, 0, k * B)
            target = stat_hbm.at[pl.ds(pl.multiple_of(row, B), B), pl.ds(pl.multiple_of(place, B), B)]
            found.append(pltpu.make_async_copy(mirror_ref.at[2 * j + k], target, sems.at[2 * j + k]))
        return found

    stores = []
    for j in range(group - 1):
        stores += mirrored(j)
        stores[-2].start()
        stores[-1].start()
    @pl.when(live == 0)
    def _():
        rows_ref[...] = prev_ref[...]
        for s in range(group):
            for c in range(HALF):
                a_ref[s * B : (s + 1) * B, c * B : (c + 1) * B] = pieces_ref[
                    s, (2 + c) * B : (3 + c) * B, :
                ]
        held = slice(0, group * B)
        store = pltpu.make_async_copy(a_ref.at[held, :], update_hbm.at[held, :], done)
        store.start()
        store.wait()

    @pl.when(live != 0)
    def _():
        def fill(block, row, col, mirror=True):
            a_ref[row : row + B, col : col + B] = block
            if mirror:
                a_ref[col : col + B, row : row + B] = block.T

        for s in range(group):
            at = s * step
            block = [pieces_ref[s, k * B : (k + 1) * B, :] for k in range(PIECE)]
            fill(block[0], at, at, False)
            fill(block[1], at, at + B)
            fill(block[2], at + B, at + B, False)
            k = 3
            for h in range(group):
                if h > s:
                    fill(block[k], at, h * step)
                    fill(block[k + 1], at, h * step + B)
                if h < s:
                    fill(block[k], at, h * step + B)
                    fill(block[k + 1], at + B, h * step + B)
                if h != s:
                    k += 2

        def power(_, carry):
            vector, _ = carry
            image = dot(vector.astype(jnp.bfloat16), a_ref[...])
            length = jnp.sqrt(jnp.sum(image * image, axis=1, keepdims=True))
            return image / length, length

        vector = jnp.full((16, order), 1.0 / math.sqrt(order), jnp.float32)
        length = jnp.ones((16, 1), jnp.float32)
        _, length = lax.fori_loop(0, POWER, power, (vector, length))
        scaling = 2.5 / length[:1, :1]
        quarter = jnp.sqrt(jnp.sqrt(scaling)) * 0.25

        def rows_of(i):
            return pl.ds(pl.multiple_of(i * step, step), step)

        def first(i, _):
            here = rows_of(i)
            line = lax.broadcasted_iota(jnp.int32, (step, order), 0) + i * step
            eye = line == lax.broadcasted_iota(jnp.int32, (step, order), 1)
            moment = scaling * a_ref[here, :].astype(jnp.float32)
            f_ref[here, :] = ((jnp.where(eye, 5.0, 0.0) - moment) * 0.25).astype(jnp.bfloat16)
            return 0

        lax.fori_loop(0, order // step, first, 0)

        def second(i, _):
            here = rows_of(i)
            factor = f_ref[here, :]
            square = dot(factor, f_ref[...])
            g_ref[here, :] = square.astype(jnp.bfloat16)
            h_ref[here, :] = (5.0 * factor.astype(jnp.float32) - 4.0 * square).astype(jnp.bfloat16)
            return 0

        lax.fori_loop(0, order // step, second, 0)

        def third(i, _):
            here = rows_of(i)
            a_ref[here, :] = dot(g_ref[here, :], g_ref[...]).astype(jnp.bfloat16)
            return 0

        lax.fori_loop(0, order // step, third, 0)

        def last(i, _):
            here = rows_of(i)
            tail = dot(a_ref[here, :], h_ref[...])
            factor = f_ref[here, :].astype(jnp.float32)
            g_ref[here, :] = ((5.0 * factor - tail) * quarter).astype(jnp.bfloat16)
            return 0

        lax.fori_loop(0, order // step, last, 0)
        rows_ref[...] = g_ref[rows_of(me), :]
        load.wait()

        def line(i, _):
            here = rows_of(i)
            f_ref[here, :] = dot(grad_ref[here, :], g_ref[...]).astype(jnp.bfloat16)
            pltpu.make_async_copy(f_ref.at[here, :], update_hbm.at[here, :], done).start()
            return 0

        lax.fori_loop(0, order // step, line, 0)
        pltpu.make_async_copy(f_ref, update_hbm, done).wait()

    for store in stores:
        store.wait()


def inverse_root(flags, pieces, prev, grad, part):
    group = pieces.shape[0]
    wide, order = grad.shape
    square = pltpu.VMEM((order, order), jnp.bfloat16)
    anywhere = pl.BlockSpec(memory_space=pl.ANY)
    return pl.pallas_call(
        functools.partial(root_kernel, group),
        in_specs=[smem(), vmem(), vmem(), anywhere, anywhere],
        out_specs=(anywhere, vmem(), anywhere),
        out_shape=(
            jax.ShapeDtypeStruct(part.shape, jnp.float32),
            jax.ShapeDtypeStruct(prev.shape, jnp.bfloat16),
            jax.ShapeDtypeStruct(grad.shape, jnp.bfloat16),
        ),
        input_output_aliases={4: 0},
        scratch_shapes=[square] * 4
        + [
            pltpu.VMEM(grad.shape, jnp.bfloat16),
            pltpu.VMEM((2 * (group - 1), B, B), jnp.float32),
            pltpu.SemaphoreType.DMA((2 * group,)),
        ],
        compiler_params=params(60),
        cost_estimate=cost(10 * order**3, 8 * MIB),
        name="root",
    )(flags, pieces, prev, grad, part)


def kept_kernel(
    group, flags_ref, late_hbm, grad_hbm, old_hbm, update_hbm, late_ref, grad_ref, half_ref, whole_ref, new_ref, sems
):
    live = flags_ref[1]
    step = 2 * B

    @pl.when(live == 0)
    def _():
        loads = [
            pltpu.make_async_copy(late_hbm, late_ref, sems.at[2]),
            pltpu.make_async_copy(old_hbm.at[: group * B, :], half_ref, sems.at[0]),
            pltpu.make_async_copy(grad_hbm, grad_ref, sems.at[3]),
        ]
        for load in loads:
            load.start()
        loads[0].wait()
        for s in range(group):
            whole_ref[s * step : s * step + B, :] = late_ref[s]
        loads[1].wait()
        for s in range(group):
            whole_ref[s * step + B : (s + 1) * step, :] = half_ref[s * B : (s + 1) * B, :]
        loads[2].wait()

        def line(i, _):
            here = pl.ds(pl.multiple_of(i * step, step), step)
            new_ref[here, :] = dot(grad_ref[here, :], whole_ref[...]).astype(jnp.bfloat16)
            pltpu.make_async_copy(new_ref.at[here, :], update_hbm.at[here, :], sems.at[1]).start()
            return 0

        lax.fori_loop(0, grad_ref.shape[0] // step, line, 0)
        pltpu.make_async_copy(new_ref, update_hbm, sems.at[1]).wait()


def kept_update(flags, late, grad, update):
    group = late.shape[0]
    wide, order = grad.shape
    anywhere = pl.BlockSpec(memory_space=pl.ANY)
    square = pltpu.VMEM((order, order), jnp.bfloat16)
    return pl.pallas_call(
        functools.partial(kept_kernel, group),
        in_specs=[smem(), anywhere, anywhere, anywhere],
        out_specs=anywhere,
        out_shape=jax.ShapeDtypeStruct(grad.shape, jnp.bfloat16),
        input_output_aliases={3: 0},
        scratch_shapes=[
            pltpu.VMEM(late.shape, jnp.bfloat16),
            pltpu.VMEM(grad.shape, jnp.bfloat16),
            pltpu.VMEM((group * B, order), jnp.bfloat16),
            square,
            pltpu.VMEM(grad.shape, jnp.bfloat16),
            pltpu.SemaphoreType.DMA((4,)),
        ],
        compiler_params=params(60),
        cost_estimate=cost(2 * wide * order * order, 8 * MIB),
        name="kept",
    )(flags, late, grad, update)


def body(tokens, cotangent, routing, stat_prev, root_prev, owner_map):
    experts = lax.axis_size("expert")
    group = lax.axis_size("group")
    my_expert = lax.axis_index("expert")
    me = lax.axis_index("group").astype(jnp.int32)
    rows, wide = tokens.shape
    order = cotangent.shape[1]
    owners = experts // 4
    live = (jnp.take(owner_map, my_expert) < owners).astype(jnp.int32)
    flags = jnp.stack([me, live])

    prev = root_prev[0]
    sent = dispatch(routing.reshape(1, rows), tokens, cotangent, experts)
    sent = sent.reshape(experts, SLOTS, wide + order)
    got = lax.all_to_all(sent, "expert", 0, 0, tiled=True)
    grad, part = gradient(got.reshape(experts * SLOTS, -1), group, wide, 1.0 / math.sqrt(rows))
    part, later = lax.optimization_barrier((part, prev))
    parts = lax.all_to_all(part, "group", 0, 0, tiled=True)
    late = jnp.broadcast_to(later[:B][None], (group, B, order))
    parts, late = lax.optimization_barrier((parts, late))
    stat_own, send = new_statistic(flags, parts, stat_prev[0], prev, wide * group)
    pieces = lax.all_to_all(send, "group", 0, 0, tiled=True)
    pieces, late = lax.optimization_barrier((pieces, late))
    late = lax.all_to_all(late, "group", 0, 0, tiled=True)
    stat, root_rows, update = inverse_root(flags, pieces, prev, grad, stat_own)
    update = kept_update(flags, late, grad, update)
    return stat[None], root_rows[None], update[None]


def solution(mesh):
    in_specs = (
        P("expert", "group"),
        P("expert", None),
        P("expert", None),
        P("expert", "group", None),
        P("expert", "group", None),
        P(),
    )
    out_specs = (P("expert", "group", None), P("expert", "group", None), P("expert", "group", None))
    return jax.shard_map(body, mesh=mesh, in_specs=in_specs, out_specs=out_specs, check_vma=False)
```

time: 244 us -> 235 us (0.963); the launches traced: 243 us -> 231 us
  waiting for transfers between devices: 66.7 us -> 43.5 us
  Pallas kernels: 16.1 us -> 24.9 us
  blocking collectives: 146 us -> 150 us
  local copies, waits for them, and re-layouts: 5.15 us -> 2.67 us
    ppermute x3 -> x0, waiting for transfers between devices: 41.7 us -> none  [body(): prevs.append(lax.ppermute(prev, 'group', ring))]
    all_to_all x0 -> x1, waiting for transfers between devices: none -> 18.5 us  [body(): late = lax.all_to_all(late, 'group', 0, 0, tiled=True)]
    all_to_all x0 -> x1, starting transfers between devices: none -> 5.3 us  [body(): late = lax.all_to_all(late, 'group', 0, 0, tiled=True)]
    ppermute x3 -> x0, starting transfers between devices: 4.18 us -> none  [body(): prevs.append(lax.ppermute(prev, 'group', ring))]
    pallas_call x2, Pallas kernels: 8.18 us -> 12.3 us  [the longest x1 6.57 us: kept_update(): pl.pallas_call(functools.partial(kept_kernel, group), in_specs=[smem(), a...]
    all_to_all x1, blocking collectives: 33 us -> 36.5 us  [body(): pieces = lax.all_to_all(send, 'group', 0, 0, tiled=True)]
    unnamed x16 -> x10, local copies, waits for them, and re-layouts: 4.41 us -> 0.99 us
  transfers between devices with their start and end apart: 4 -> 2, of which waited for: 4 -> 2; matrix products, arithmetic and copies ran while one was open for 0% -> 0% of each run, Pallas kernels for 1% -> 2%
where the time goes in v2:
time: 235 us; the launch traced here: 231 us
  blocking collectives  150 us (64%)
  waiting for transfers between devices  43.5 us (19%)
  Pallas kernels  24.9 us (11%)
  starting transfers between devices  9.19 us (4%)
  local copies, waits for them, and re-layouts  2.67 us (1%)
    all_to_all x1, blocking collectives, body(): got = lax.all_to_all(sent, 'expert', 0, 0, tiled=True)  113 us
    all_to_all x1, blocking collectives, body(): pieces = lax.all_to_all(send, 'group', 0, 0, tiled=True)  36.5 us
    all_to_all x1, waiting for transfers between devices, body(): parts = lax.all_to_all(part, 'group', 0, 0, tiled=True)  25 us
    all_to_all x1, waiting for transfers between devices, body(): late = lax.all_to_all(late, 'group', 0, 0, tiled=True)  18.5 us
    pallas_call x1, Pallas kernels, gradient(): pl.pallas_call(functools.partial(gradient_kernel, group, scale), in_specs...  7.05 us
    pallas_call x1, Pallas kernels, kept_update(): pl.pallas_call(functools.partial(kept_kernel, group), in_specs=[smem(), a...  6.57 us
    pallas_call x1, Pallas kernels, dispatch(): pl.pallas_call(functools.partial(dispatch_kernel, experts), grid=(total /...  5.7 us
    all_to_all x1, starting transfers between devices, body(): late = lax.all_to_all(late, 'group', 0, 0, tiled=True)  5.3 us
  transfers between devices with their start and end apart: 2, of which 2 were waited for; matrix products, arithmetic and copies ran while one was open for 0% of the time, Pallas kernels for 2%

profile of v2, /device:TPU:32, one launch (start us, length us, event | category | flops | bytes accessed | tf_op | source)
XLA Modules:
  0.0 231.4 jit_solution(13067183790134129710)
XLA Ops:
  0.6 5.7 %dispatch.1 = bf16[1024,2048]{1,0:T(8,128)(2,1)} custom-call(s32[1,480]{1,0:T(1,128)} %bitcast.17, bf16[480,1024]{1,0:T(8,128)(2,1)} %tok_hbm.1, bf16[480,1024]{1,0:T(8,128)(2,1)} %sig_hbm.1), custom_call_target="tpu_custom_call" | custom-call | flops 2013265920 | bytes 6291456 | tf_op jit(solution)/shard_map/dispatch/pallas_call | solution.py:85
  6.3 113.2 %all_to_all.20 = bf16[64,16,2048]{2,1,0:T(8,128)(2,1)} all-to-all(bf16[64,16,2048]{2,1,0:T(8,128)(2,1)} %bitcast.15), channel_id=1, replica_groups=mesh['expert'=64,'group'=4] {'expert'}, dimensions={0} | all-to-all | bytes 8388608 | tf_op jit(solution)/shard_map/all_to_all | solution.py:512
  119.5 7.1 %gradient.1 = (bf16[1024,1024]{1,0:T(8,128)(2,1)}, bf16[4,1152,128]{2,1,0:T(8,128)(2,1)}) custom-call(bf16[1024,2048]{1,0:T(8,128)(2,1)} %bitcast.14), custom_call_target="tpu_custom_call" | custom-call | flops 4294967296 | bytes 10485760 | tf_op jit(solution)/shard_map/gradient/pallas_call | solution.py:162
  126.6 0.0 copy-start.4
  126.6 0.0 copy-start
  126.6 0.0 copy-start.1
  126.6 3.9 %all-to-all-start.1 = ((bf16[4,1152,128]{2,1,0:T(8,128)(2,1)}), bf16[4,1152,128]{2,1,0:T(8,128)(2,1)S(1)}, u32[]{:S(2)}, u32[]{:S(2)}) async-start(bf16[4,1152,128]{2,1,0:T(8,128)(2,1)} %get-tuple-element.17), calls=%async_computation.1 | async-start | bytes 2359296 | tf_op jit(solution)/shard_map/all_to_all | solution.py:515
  130.5 0.0 copy-done.4
  130.5 0.6 dynamic-slice.2
  131.8 0.1 pad_add_fusion.flags_ref
  131.8 0.0 copy-done
  131.8 0.0 copy-start.2
  131.9 25.0 %all-to-all-done.1.parts_ref = bf16[4,1152,128]{2,1,0:T(8,128)(2,1)S(1)} async-done(((bf16[4,1152,128]{2,1,0:T(8,128)(2,1)}), bf16[4,1152,128]{2,1,0:T(8,128)(2,1)S(1)}, u32[]{:S(2)}, u32[]{:S(2)}) %all-to-all-start.1) | async-done | bytes 1179680 | tf_op jit(solution)/shard_map/all_to_all | solution.py:515
  156.9 1.1 broadcast_in_dim.20
  158.0 0.0 copy-done.1
  158.0 1.9 statistic.1
  159.9 0.0 copy-done.2
  159.9 36.5 %all_to_all.21.pieces_ref = bf16[4,1280,128]{2,1,0:T(8,128)(2,1)} all-to-all(bf16[4,1280,128]{2,1,0:T(8,128)(2,1)S(1)} %get-tuple-element.20), channel_id=1, replica_groups=mesh['expert'=64,'group'=4] {'group'}, dimensions={0} | all-to-all | bytes 2621440 | tf_op jit(solution)/shard_map/all_to_all | solution.py:519
  196.4 5.3 %all-to-all-start.3 = ((bf16[4,128,1024]{2,1,0:T(8,128)(2,1)}), bf16[4,128,1024]{2,1,0:T(8,128)(2,1)S(1)}, u32[]{:S(2)}, u32[]{:S(2)}) async-start(bf16[4,128,1024]{2,1,0:T(8,128)(2,1)} %broadcast_in_dim.20), calls=%async_computation.3 | async-start | bytes 2097152 | tf_op jit(solution)/shard_map/all_to_all | solution.py:521
  201.7 3.7 %root.1 = (f32[256,1024]{1,0:T(8,128)}, bf16[256,1024]{1,0:T(8,128)(2,1)}, bf16[1024,1024]{1,0:T(8,128)(2,1)}) custom-call(s32[2]{0:T(128)} %copy-done.2, bf16[4,1280,128]{2,1,0:T(8,128)(2,1)} %all_to_all.21.pieces_ref, bf16[256,1024]{1,0:T(8,128)(2,1)} %bitcast.10, bf16[1024,1024]{1,0:T(8,128)(2,1)} %get-tuple-element.23.grad_hbm, ...), custom_call_target="tpu_custom_call", output_to_operand_aliasing={{0}: (4, {})} | custom-call | flops 10737418240 | bytes 8388608 | tf_op jit(solution)/shard_map/root/pallas_call | solution.py:418
  205.4 18.5 %all-to-all-done.3.late_hbm = bf16[4,128,1024]{2,1,0:T(8,128)(2,1)S(1)} async-done(((bf16[4,128,1024]{2,1,0:T(8,128)(2,1)}), bf16[4,128,1024]{2,1,0:T(8,128)(2,1)S(1)}, u32[]{:S(2)}, u32[]{:S(2)}) %all-to-all-start.3) | async-done | bytes 1048608 | tf_op jit(solution)/shard_map/all_to_all | solution.py:521
  223.9 0.0 copy-start.3
  223.9 1.0 copy-done.3
  224.8 6.6 %kept.1 = bf16[1024,1024]{1,0:T(8,128)(2,1)} custom-call(s32[2]{0:T(128)} %copy-done.2, bf16[4,128,1024]{2,1,0:T(8,128)(2,1)} %copy-done.3, bf16[1024,1024]{1,0:T(8,128)(2,1)} %get-tuple-element.23.grad_hbm, bf16[1024,1024]{1,0:T(8,128)(2,1)} %get-tuple-element.28.old_hbm), custom_call_target="tpu_custom_call", output_to_operand_aliasing={{}: (3, {})} | custom-call | flops 2147483648 | bytes 8388608 | tf_op jit(solution)/shard_map/kept/pallas_call | solution.py:478
  (1 shorter events, 0.0 us)
Async XLA Ops:
  126.6 3.9 %copy-start.4 = (s32[64]{0:T(128)S(1)}, s32[64]{0:T(128)}, u32[]{:S(2)}) copy-start(s32[64]{0:T(128)} %param.11) | copy-start | bytes 772
  126.6 5.2 %copy-start = (bf16[1,256,1024]{2,1,0:T(8,128)(2,1)S(1)}, bf16[1,256,1024]{2,1,0:T(8,128)(2,1)}, u32[]{:S(2)}) copy-start(bf16[1,256,1024]{2,1,0:T(8,128)(2,1)} %param.10) | copy-start | bytes 1572868
  126.6 31.4 %copy-start.1 = (f32[1,256,1024]{2,1,0:T(8,128)S(1)}, f32[1,256,1024]{2,1,0:T(8,128)}, u32[]{:S(2)}) copy-start(f32[1,256,1024]{2,1,0:T(8,128)} %param.9) | copy-start | bytes 3145732
  126.6 30.3 %all-to-all-start.1 = ((bf16[4,1152,128]{2,1,0:T(8,128)(2,1)}), bf16[4,1152,128]{2,1,0:T(8,128)(2,1)S(1)}, u32[]{:S(2)}, u32[]{:S(2)}) async-start(bf16[4,1152,128]{2,1,0:T(8,128)(2,1)} %get-tuple-element.17), calls=%async_computation.1 | async-start | bytes 2359296 | tf_op jit(solution)/shard_map/all_to_all | solution.py:515
  131.8 28.1 %copy-start.2 = (s32[2]{0:T(128)}, s32[2]{0:T(128)S(1)}, u32[]{:S(2)}) copy-start(s32[2]{0:T(128)S(1)} %pad_add_fusion.flags_ref) | copy-start | bytes 28
  196.4 27.5 %all-to-all-start.3 = ((bf16[4,128,1024]{2,1,0:T(8,128)(2,1)}), bf16[4,128,1024]{2,1,0:T(8,128)(2,1)S(1)}, u32[]{:S(2)}, u32[]{:S(2)}) async-start(bf16[4,128,1024]{2,1,0:T(8,128)(2,1)} %broadcast_in_dim.20), calls=%async_computation.3 | async-start | bytes 2097152 | tf_op jit(solution)/shard_map/all_to_all | solution.py:521
  223.9 1.0 copy-start.3

commit v3 on v2

--- a/solution.py
+++ b/solution.py
@@ -7,6 +7,7 @@
 from jax.experimental import pallas as pl
 from jax.experimental.pallas import tpu as pltpu
 from jax.sharding import PartitionSpec as P
+
 
 POWER = 8
 KEEP = 0.9
@@ -307,6 +308,7 @@
         stores += mirrored(j)
         stores[-2].start()
         stores[-1].start()
+
     @pl.when(live == 0)
     def _():
         rows_ref[...] = prev_ref[...]
@@ -412,7 +414,7 @@
 
 def inverse_root(flags, pieces, prev, grad, part):
     group = pieces.shape[0]
-    wide, order = grad.shape
+    _, order = grad.shape
     square = pltpu.VMEM((order, order), jnp.bfloat16)
     anywhere = pl.BlockSpec(memory_space=pl.ANY)
     return pl.pallas_call(
@@ -438,64 +440,64 @@
 
 
 def kept_kernel(
-    group, flags_ref, late_hbm, grad_hbm, old_hbm, update_hbm, late_ref, grad_ref, half_ref, whole_ref, new_ref, sems
+    group, flags_ref, first_hbm, prev_hbm, second_hbm, third_hbm, grad_hbm, old_hbm, update_hbm, *scratch
 ):
-    live = flags_ref[1]
+    upper_ref, grad_ref, half_ref, whole_ref, new_ref, sems = scratch
+    me, live = flags_ref[0], flags_ref[1]
     step = 2 * B
 
     @pl.when(live == 0)
     def _():
-        loads = [
-            pltpu.make_async_copy(late_hbm, late_ref, sems.at[2]),
-            pltpu.make_async_copy(old_hbm.at[: group * B, :], half_ref, sems.at[0]),
-            pltpu.make_async_copy(grad_hbm, grad_ref, sems.at[3]),
-        ]
+        uppers = (prev_hbm.at[:B, :], first_hbm, second_hbm, third_hbm)
+        loads = [pltpu.make_async_copy(uppers[k], upper_ref.at[k], sems.at[k]) for k in range(group)]
+        loads.append(pltpu.make_async_copy(old_hbm.at[: group * B, :], half_ref, sems.at[group]))
+        loads.append(pltpu.make_async_copy(grad_hbm, grad_ref, sems.at[group + 1]))
         for load in loads:
             load.start()
-        loads[0].wait()
-        for s in range(group):
-            whole_ref[s * step : s * step + B, :] = late_ref[s]
-        loads[1].wait()
+        for k in range(group):
+            loads[k].wait()
+            source = lax.rem(me - k + group, group)
+            whole_ref[pl.ds(pl.multiple_of(source * step, step), B), :] = upper_ref[k]
+        loads[group].wait()
         for s in range(group):
             whole_ref[s * step + B : (s + 1) * step, :] = half_ref[s * B : (s + 1) * B, :]
-        loads[2].wait()
+        loads[group + 1].wait()
 
         def line(i, _):
             here = pl.ds(pl.multiple_of(i * step, step), step)
             new_ref[here, :] = dot(grad_ref[here, :], whole_ref[...]).astype(jnp.bfloat16)
-            pltpu.make_async_copy(new_ref.at[here, :], update_hbm.at[here, :], sems.at[1]).start()
+            pltpu.make_async_copy(new_ref.at[here, :], update_hbm.at[here, :], sems.at[group + 2]).start()
             return 0
 
         lax.fori_loop(0, grad_ref.shape[0] // step, line, 0)
-        pltpu.make_async_copy(new_ref, update_hbm, sems.at[1]).wait()
-
-
-def kept_update(flags, late, grad, update):
-    group = late.shape[0]
+        pltpu.make_async_copy(new_ref, update_hbm, sems.at[group + 2]).wait()
+
+
+def kept_update(flags, first, prev, second, third, grad, update):
+    group = 4
     wide, order = grad.shape
     anywhere = pl.BlockSpec(memory_space=pl.ANY)
-    square = pltpu.VMEM((order, order), jnp.bfloat16)
     return pl.pallas_call(
         functools.partial(kept_kernel, group),
-        in_specs=[smem(), anywhere, anywhere, anywhere],
+        in_specs=[smem()] + [anywhere] * 6,
         out_specs=anywhere,
         out_shape=jax.ShapeDtypeStruct(grad.shape, jnp.bfloat16),
-        input_output_aliases={3: 0},
+        input_output_aliases={6: 0},
         scratch_shapes=[
-            pltpu.VMEM(late.shape, jnp.bfloat16),
+            pltpu.VMEM((group, B, order), jnp.bfloat16),
             pltpu.VMEM(grad.shape, jnp.bfloat16),
             pltpu.VMEM((group * B, order), jnp.bfloat16),
-            square,
+            pltpu.VMEM((order, order), jnp.bfloat16),
             pltpu.VMEM(grad.shape, jnp.bfloat16),
-            pltpu.SemaphoreType.DMA((4,)),
+            pltpu.SemaphoreType.DMA((group + 3,)),
         ],
         compiler_params=params(60),
         cost_estimate=cost(2 * wide * order * order, 8 * MIB),
         name="kept",
-    )(flags, late, grad, update)
-
-
-def body(tokens, cotangent, routing, stat_prev, root_prev, owner_map):
+    )(flags, first, prev, second, third, grad, update)
+
+
+def step_of(tokens, cotangent, routing, stat_prev, root_prev, owner_map):
     experts = lax.axis_size("expert")
     group = lax.axis_size("group")
     my_expert = lax.axis_index("expert")
@@ -506,21 +508,24 @@
     live = (jnp.take(owner_map, my_expert) < owners).astype(jnp.int32)
     flags = jnp.stack([me, live])
 
+    def shifted(x, k):
+        return lax.ppermute(x, "group", [(g, (g + k) % group) for g in range(group)])
+
     prev = root_prev[0]
+    upper = prev[:B]
+    from_1 = shifted(upper, 1)
+    from_3 = shifted(upper, 3)
     sent = dispatch(routing.reshape(1, rows), tokens, cotangent, experts)
     sent = sent.reshape(experts, SLOTS, wide + order)
     got = lax.all_to_all(sent, "expert", 0, 0, tiled=True)
     grad, part = gradient(got.reshape(experts * SLOTS, -1), group, wide, 1.0 / math.sqrt(rows))
-    part, later = lax.optimization_barrier((part, prev))
     parts = lax.all_to_all(part, "group", 0, 0, tiled=True)
-    late = jnp.broadcast_to(later[:B][None], (group, B, order))
-    parts, late = lax.optimization_barrier((parts, late))
     stat_own, send = new_statistic(flags, parts, stat_prev[0], prev, wide * group)
     pieces = lax.all_to_all(send, "group", 0, 0, tiled=True)
-    pieces, late = lax.optimization_barrier((pieces, late))
-    late = lax.all_to_all(late, "group", 0, 0, tiled=True)
+    pieces, upper = lax.optimization_barrier((pieces, upper))
+    from_2 = shifted(upper, 2)
     stat, root_rows, update = inverse_root(flags, pieces, prev, grad, stat_own)
-    update = kept_update(flags, late, grad, update)
+    update = kept_update(flags, from_1, prev, from_2, from_3, grad, update)
     return stat[None], root_rows[None], update[None]
 
 
@@ -534,4 +539,4 @@
         P(),
     )
     out_specs = (P("expert", "group", None), P("expert", "group", None), P("expert", "group", None))
-    return jax.shard_map(body, mesh=mesh, in_specs=in_specs, out_specs=out_specs, check_vma=False)
+    return jax.shard_map(step_of, mesh=mesh, in_specs=in_specs, out_specs=out_specs, check_vma=False)

time: 235 us -> 230 us (0.979)
  blocking collectives: 150 us -> 113 us
  waiting for transfers between devices: 43.5 us -> 66.9 us
  starting transfers between devices: 9.19 us -> 16.8 us
    all_to_all x2 -> x1, blocking collectives: 150 us -> 113 us  [step_of(): got = lax.all_to_all(sent, 'expert', 0, 0, tiled=True)]
    all_to_all x2, waiting for transfers between devices: 43.5 us -> 58 us  [the longest x1 33 us: step_of(): pieces = lax.all_to_all(send, 'group', 0, 0, tiled=True)]
    ppermute x0 -> x3, waiting for transfers between devices: none -> 8.87 us  [shifted(): lax.ppermute(x, 'group', [(g, (g + k) % group) for g in range(group)])]
    ppermute x0 -> x3, starting transfers between devices: none -> 5.48 us  [shifted(): lax.ppermute(x, 'group', [(g, (g + k) % group) for g in range(group)])]
  transfers between devices with their start and end apart: 2 -> 5, of which waited for: 2 -> 5; matrix products, arithmetic and copies ran while one was open for 0% -> 0% of each run, Pallas kernels for 2% -> 2%
where the time goes in v3:
time: 230 us; the launch traced here: 226 us
  blocking collectives  113 us (49%)
  waiting for transfers between devices  66.9 us (29%)
  Pallas kernels  26.1 us (11%)
  starting transfers between devices  16.8 us (7%)
    all_to_all x1, blocking collectives, step_of(): got = lax.all_to_all(sent, 'expert', 0, 0, tiled=True)  113 us
    all_to_all x1, waiting for transfers between devices, step_of(): pieces = lax.all_to_all(send, 'group', 0, 0, tiled=True)  33 us
    all_to_all x1, waiting for transfers between devices, step_of(): parts = lax.all_to_all(part, 'group', 0, 0, tiled=True)  25 us
    ppermute x3, waiting for transfers between devices, shifted(): lax.ppermute(x, 'group', [(g, (g + k) % group) for g in range(group)])  8.87 us
    all_to_all x1, starting transfers between devices, step_of(): pieces = lax.all_to_all(send, 'group', 0, 0, tiled=True)  7.48 us
    pallas_call x1, Pallas kernels, gradient(): pl.pallas_call(functools.partial(gradient_kernel, group, scale), in_specs...  7.05 us
    pallas_call x1, Pallas kernels, kept_update(): pl.pallas_call(functools.partial(kept_kernel, group), in_specs=[smem()] +...  6.61 us
    pallas_call x1, Pallas kernels, dispatch(): pl.pallas_call(functools.partial(dispatch_kernel, experts), grid=(total /...  5.74 us
  transfers between devices with their start and end apart: 5, of which 5 were waited for; matrix products, arithmetic and copies ran while one was open for 0% of the time, Pallas kernels for 2%

profile of v3, /device:TPU:32, one launch (start us, length us, event | category | flops | bytes accessed | tf_op | source)
XLA Modules:
  0.0 225.7 jit_solution(4306699842461287010)
XLA Ops:
  0.6 5.7 %dispatch.1 = bf16[1024,2048]{1,0:T(8,128)(2,1)} custom-call(s32[1,480]{1,0:T(1,128)} %bitcast.19, bf16[480,1024]{1,0:T(8,128)(2,1)} %tok_hbm.1, bf16[480,1024]{1,0:T(8,128)(2,1)} %sig_hbm.1), custom_call_target="tpu_custom_call" | custom-call | flops 2013265920 | bytes 6291456 | tf_op jit(solution)/shard_map/dispatch/pallas_call | solution.py:86
  6.4 113.2 %all_to_all.15 = bf16[64,16,2048]{2,1,0:T(8,128)(2,1)} all-to-all(bf16[64,16,2048]{2,1,0:T(8,128)(2,1)} %bitcast.17), channel_id=1, replica_groups=mesh['expert'=64,'group'=4] {'expert'}, dimensions={0} | all-to-all | bytes 8388608 | tf_op jit(solution)/shard_map/all_to_all | solution.py:520
  119.6 7.0 %gradient.1 = (bf16[1024,1024]{1,0:T(8,128)(2,1)}, bf16[4,1152,128]{2,1,0:T(8,128)(2,1)}) custom-call(bf16[1024,2048]{1,0:T(8,128)(2,1)} %bitcast.16), custom_call_target="tpu_custom_call" | custom-call | flops 4294967296 | bytes 10485760 | tf_op jit(solution)/shard_map/gradient/pallas_call | solution.py:163
  126.6 0.0 copy-start.6
  126.6 0.0 copy-start
  126.7 0.0 copy-start.1
  126.7 3.9 %all-to-all-start.1 = ((bf16[4,1152,128]{2,1,0:T(8,128)(2,1)}), bf16[4,1152,128]{2,1,0:T(8,128)(2,1)S(1)}, u32[]{:S(2)}, u32[]{:S(2)}) async-start(bf16[4,1152,128]{2,1,0:T(8,128)(2,1)} %get-tuple-element.12), calls=%async_computation.1 | async-start | bytes 2359296 | tf_op jit(solution)/shard_map/all_to_all | solution.py:522
  130.5 0.0 copy-done.6
  130.5 0.6 dynamic-slice.2
  131.8 0.1 pad_add_fusion.flags_ref
  131.9 0.0 copy-start.2
  131.9 25.0 %all-to-all-done.1.parts_ref = bf16[4,1152,128]{2,1,0:T(8,128)(2,1)S(1)} async-done(((bf16[4,1152,128]{2,1,0:T(8,128)(2,1)}), bf16[4,1152,128]{2,1,0:T(8,128)(2,1)S(1)}, u32[]{:S(2)}, u32[]{:S(2)}) %all-to-all-start.1) | async-done | bytes 1179680 | tf_op jit(solution)/shard_map/all_to_all | solution.py:522
  156.9 0.0 copy-done
  156.9 0.0 copy-done.1
  156.9 3.0 %statistic.1 = (f32[256,1024]{1,0:T(8,128)}, bf16[4,1280,128]{2,1,0:T(8,128)(2,1)}) custom-call(s32[2]{0:T(128)S(1)} %pad_add_fusion.flags_ref, bf16[4,1152,128]{2,1,0:T(8,128)(2,1)S(1)} %all-to-all-done.1.parts_ref, f32[256,1024]{1,0:T(8,128)S(1)} %bitcast.15, bf16[256,1024]{1,0:T(8,128)(2,1)S(1)} %bitcast.14), custom_call_target="tpu_custom_call" | custom-call | flops 1048576 | bytes 4194304 | tf_op jit(solution)/shard_map/statistic/pallas_call | solution.py:245
  159.9 0.0 copy-done.2
  159.9 7.5 %all-to-all-start.2 = ((bf16[4,1280,128]{2,1,0:T(8,128)(2,1)}), bf16[4,1280,128]{2,1,0:T(8,128)(2,1)}, u32[]{:S(2)}, u32[]{:S(2)}) async-start(bf16[4,1280,128]{2,1,0:T(8,128)(2,1)} %get-tuple-element.13), calls=%async_computation.2 | async-start | bytes 2621440 | tf_op jit(solution)/shard_map/all_to_all | solution.py:524
  167.4 1.5 collective-permute-start
  168.9 0.6 collective-permute-start.2
  169.5 33.0 %all-to-all-done.2.pieces_ref = bf16[4,1280,128]{2,1,0:T(8,128)(2,1)} async-done(((bf16[4,1280,128]{2,1,0:T(8,128)(2,1)}), bf16[4,1280,128]{2,1,0:T(8,128)(2,1)}, u32[]{:S(2)}, u32[]{:S(2)}) %all-to-all-start.2) | async-done | bytes 1310752 | tf_op jit(solution)/shard_map/all_to_all | solution.py:524
  202.5 3.4 %collective-permute-start.1 = (bf16[128,1024]{1,0:T(8,128)(2,1)S(1)}, bf16[128,1024]{1,0:T(8,128)(2,1)S(1)}, u32[]{:S(2)}, u32[]{:S(2)}) collective-permute-start(bf16[128,1024]{1,0:T(8,128)(2,1)S(1)} %slice_bitcast_fusion), channel_id=1, source_target_pairs={{0,2},{1,3},{2,0},{3,1},{4,6},{5,7},{6,4},{7,5},{8,10},{9,11},{10,... | collective-permute-start | bytes 786440 | tf_op jit(solution)/shard_map/ppermute | solution.py:512
  205.8 3.7 %root.1 = (f32[256,1024]{1,0:T(8,128)}, bf16[256,1024]{1,0:T(8,128)(2,1)}, bf16[1024,1024]{1,0:T(8,128)(2,1)}) custom-call(s32[2]{0:T(128)} %copy-done.2, bf16[4,1280,128]{2,1,0:T(8,128)(2,1)} %all-to-all-done.2.pieces_ref, bf16[256,1024]{1,0:T(8,128)(2,1)} %bitcast.12, ...), custom_call_target="tpu_custom_call", output_to_operand_aliasing={{0}: (4, {})} | custom-call | flops 10737418240 | bytes 8388608 | tf_op jit(solution)/shard_map/root/pallas_call | solution.py:420
  209.5 4.1 %collective-permute-done.first_hbm = bf16[128,1024]{1,0:T(8,128)(2,1)S(1)} collective-permute-done((bf16[128,1024]{1,0:T(8,128)(2,1)S(1)}, bf16[128,1024]{1,0:T(8,128)(2,1)S(1)}, u32[]{:S(2)}, u32[]{:S(2)}) %collective-permute-start) | collective-permute-done | bytes 262176 | tf_op jit(solution)/shard_map/ppermute | solution.py:512
  213.6 0.0 copy-start.3
  213.6 1.9 collective-permute-done.2.third_hbm
  215.5 0.0 copy-start.4
  215.5 2.9 %collective-permute-done.1.second_hbm = bf16[128,1024]{1,0:T(8,128)(2,1)S(1)} collective-permute-done((bf16[128,1024]{1,0:T(8,128)(2,1)S(1)}, bf16[128,1024]{1,0:T(8,128)(2,1)S(1)}, u32[]{:S(2)}, u32[]{:S(2)}) %collective-permute-start.1) | collective-permute-done | bytes 262176 | tf_op jit(solution)/shard_map/ppermute | solution.py:512
  218.4 0.0 copy-start.5
  218.4 0.0 copy-done.3
  218.4 0.0 copy-done.4
  218.4 0.7 copy-done.5
  219.1 6.6 %kept.1 = bf16[1024,1024]{1,0:T(8,128)(2,1)} custom-call(s32[2]{0:T(128)} %copy-done.2, bf16[128,1024]{1,0:T(8,128)(2,1)} %copy-done.3, bf16[256,1024]{1,0:T(8,128)(2,1)} %bitcast.13, bf16[128,1024]{1,0:T(8,128)(2,1)} %copy-done.5, bf16[128,1024]{1,0:T(8,128)(2,1)} %copy-done.4, ...), custom_call_target="tpu_custom_call", output_to_operand_aliasing={{}: (6, {})} | custom-call | flops 2147483648 | bytes 8388608 | tf_op jit(solution)/shard_map/kept/pallas_call | solution.py:480
  (1 shorter events, 0.0 us)
Async XLA Ops:
  126.6 3.9 %copy-start.6 = (s32[64]{0:T(128)S(1)}, s32[64]{0:T(128)}, u32[]{:S(2)}) copy-start(s32[64]{0:T(128)} %param.11) | copy-start | bytes 772
  126.6 30.2 %copy-start = (bf16[1,256,1024]{2,1,0:T(8,128)(2,1)S(1)}, bf16[1,256,1024]{2,1,0:T(8,128)(2,1)}, u32[]{:S(2)}) copy-start(bf16[1,256,1024]{2,1,0:T(8,128)(2,1)} %param.10) | copy-start | bytes 1572868
  126.7 30.2 %copy-start.1 = (f32[1,256,1024]{2,1,0:T(8,128)S(1)}, f32[1,256,1024]{2,1,0:T(8,128)}, u32[]{:S(2)}) copy-start(f32[1,256,1024]{2,1,0:T(8,128)} %param.9) | copy-start | bytes 3145732
  126.7 30.2 %all-to-all-start.1 = ((bf16[4,1152,128]{2,1,0:T(8,128)(2,1)}), bf16[4,1152,128]{2,1,0:T(8,128)(2,1)S(1)}, u32[]{:S(2)}, u32[]{:S(2)}) async-start(bf16[4,1152,128]{2,1,0:T(8,128)(2,1)} %get-tuple-element.12), calls=%async_computation.1 | async-start | bytes 2359296 | tf_op jit(solution)/shard_map/all_to_all | solution.py:522
  131.9 28.0 %copy-start.2 = (s32[2]{0:T(128)}, s32[2]{0:T(128)S(1)}, u32[]{:S(2)}) copy-start(s32[2]{0:T(128)S(1)} %pad_add_fusion.flags_ref) | copy-start | bytes 28
  159.9 42.6 %all-to-all-start.2 = ((bf16[4,1280,128]{2,1,0:T(8,128)(2,1)}), bf16[4,1280,128]{2,1,0:T(8,128)(2,1)}, u32[]{:S(2)}, u32[]{:S(2)}) async-start(bf16[4,1280,128]{2,1,0:T(8,128)(2,1)} %get-tuple-element.13), calls=%async_computation.2 | async-start | bytes 2621440 | tf_op jit(solution)/shard_map/all_to_all | solution.py:524
  167.4 46.2 %collective-permute-start = (bf16[128,1024]{1,0:T(8,128)(2,1)S(1)}, bf16[128,1024]{1,0:T(8,128)(2,1)S(1)}, u32[]{:S(2)}, u32[]{:S(2)}) collective-permute-start(bf16[128,1024]{1,0:T(8,128)(2,1)S(1)} %slice_bitcast_fusion), channel_id=1, source_target_pairs={{0,1},{1,2},{2,3},{3,0},{4,5},{5,6},{6,7},{7,4},{8,9},{9,10},{10,1... | collective-permute-start | bytes 786440 | tf_op jit(solution)/shard_map/ppermute | solution.py:512
  168.9 46.6 %collective-permute-start.2 = (bf16[128,1024]{1,0:T(8,128)(2,1)S(1)}, bf16[128,1024]{1,0:T(8,128)(2,1)S(1)}, u32[]{:S(2)}, u32[]{:S(2)}) collective-permute-start(bf16[128,1024]{1,0:T(8,128)(2,1)S(1)} %slice_bitcast_fusion), channel_id=1, source_target_pairs={{0,3},{1,0},{2,1},{3,2},{4,7},{5,4},{6,5},{7,6},{8,11},{9,8},{10,9... | collective-permute-start | bytes 786440 | tf_op jit(solution)/shard_map/ppermute | solution.py:512
  202.5 15.9 %collective-permute-start.1 = (bf16[128,1024]{1,0:T(8,128)(2,1)S(1)}, bf16[128,1024]{1,0:T(8,128)(2,1)S(1)}, u32[]{:S(2)}, u32[]{:S(2)}) collective-permute-start(bf16[128,1024]{1,0:T(8,128)(2,1)S(1)} %slice_bitcast_fusion), channel_id=1, source_target_pairs={{0,2},{1,3},{2,0},{3,1},{4,6},{5,7},{6,4},{7,5},{8,10},{9,11},{10,... | collective-permute-start | bytes 786440 | tf_op jit(solution)/shard_map/ppermute | solution.py:512
  213.6 4.8 %copy-start.3 = (bf16[128,1024]{1,0:T(8,128)(2,1)}, bf16[128,1024]{1,0:T(8,128)(2,1)S(1)}, u32[]{:S(2)}) copy-start(bf16[128,1024]{1,0:T(8,128)(2,1)S(1)} %collective-permute-done.first_hbm) | copy-start | bytes 786436
  215.5 2.9 %copy-start.4 = (bf16[128,1024]{1,0:T(8,128)(2,1)}, bf16[128,1024]{1,0:T(8,128)(2,1)S(1)}, u32[]{:S(2)}) copy-start(bf16[128,1024]{1,0:T(8,128)(2,1)S(1)} %collective-permute-done.2.third_hbm) | copy-start | bytes 786436
  218.4 0.7 copy-start.5

commit v4 on v3

--- a/solution.py
+++ b/solution.py
@@ -266,6 +266,9 @@
     flags_ref,
     pieces_ref,
     prev_ref,
+    first_hbm,
+    second_hbm,
+    third_hbm,
     grad_hbm,
     part_hbm,
     stat_hbm,
@@ -276,6 +279,7 @@
     g_ref,
     h_ref,
     grad_ref,
+    upper_ref,
     mirror_ref,
     sems,
 ):
@@ -284,10 +288,16 @@
     step = 2 * B
     done = sems.at[2 * group - 2]
     load = pltpu.make_async_copy(grad_hbm, grad_ref, sems.at[2 * group - 1])
-
-    @pl.when(live != 0)
-    def _():
-        load.start()
+    uppers = [
+        pltpu.make_async_copy(source, upper_ref.at[k], sems.at[2 * group + k])
+        for k, source in enumerate((first_hbm, second_hbm, third_hbm))
+    ]
+    load.start()
+
+    @pl.when(live == 0)
+    def _():
+        for upper in uppers:
+            upper.start()
 
     def mirrored(j):
         s = jnp.where(j < me, j, j + 1)
@@ -309,18 +319,21 @@
         stores[-2].start()
         stores[-1].start()
 
+    def rows_of(i, count=step):
+        return pl.ds(pl.multiple_of(i * step, step), count)
+
     @pl.when(live == 0)
     def _():
         rows_ref[...] = prev_ref[...]
         for s in range(group):
             for c in range(HALF):
-                a_ref[s * B : (s + 1) * B, c * B : (c + 1) * B] = pieces_ref[
+                g_ref[s * step + B : (s + 1) * step, c * B : (c + 1) * B] = pieces_ref[
                     s, (2 + c) * B : (3 + c) * B, :
                 ]
-        held = slice(0, group * B)
-        store = pltpu.make_async_copy(a_ref.at[held, :], update_hbm.at[held, :], done)
-        store.start()
-        store.wait()
+        g_ref[rows_of(me, B), :] = prev_ref[:B, :]
+        for k in range(1, group):
+            uppers[k - 1].wait()
+            g_ref[rows_of(lax.rem(me - k + group, group), B), :] = upper_ref[k - 1]
 
     @pl.when(live != 0)
     def _():
@@ -358,9 +371,6 @@
         scaling = 2.5 / length[:1, :1]
         quarter = jnp.sqrt(jnp.sqrt(scaling)) * 0.25
 
-        def rows_of(i):
-            return pl.ds(pl.multiple_of(i * step, step), step)
-
         def first(i, _):
             here = rows_of(i)
             line = lax.broadcasted_iota(jnp.int32, (step, order), 0) + i * step
@@ -397,104 +407,48 @@
 
         lax.fori_loop(0, order // step, last, 0)
         rows_ref[...] = g_ref[rows_of(me), :]
-        load.wait()
-
-        def line(i, _):
-            here = rows_of(i)
-            f_ref[here, :] = dot(grad_ref[here, :], g_ref[...]).astype(jnp.bfloat16)
-            pltpu.make_async_copy(f_ref.at[here, :], update_hbm.at[here, :], done).start()
-            return 0
-
-        lax.fori_loop(0, order // step, line, 0)
-        pltpu.make_async_copy(f_ref, update_hbm, done).wait()
+
+    load.wait()
+
+    def line(i, _):
+        here = rows_of(i)
+        f_ref[here, :] = dot(grad_ref[here, :], g_ref[...]).astype(jnp.bfloat16)
+        pltpu.make_async_copy(f_ref.at[here, :], update_hbm.at[here, :], done).start()
+        return 0
+
+    lax.fori_loop(0, order // step, line, 0)
+    pltpu.make_async_copy(f_ref, update_hbm, done).wait()
 
     for store in stores:
         store.wait()
 
 
-def inverse_root(flags, pieces, prev, grad, part):
+def inverse_root(flags, pieces, prev, uppers, grad, part):
     group = pieces.shape[0]
     _, order = grad.shape
     square = pltpu.VMEM((order, order), jnp.bfloat16)
     anywhere = pl.BlockSpec(memory_space=pl.ANY)
     return pl.pallas_call(
         functools.partial(root_kernel, group),
-        in_specs=[smem(), vmem(), vmem(), anywhere, anywhere],
+        in_specs=[smem(), vmem(), vmem()] + [anywhere] * 5,
         out_specs=(anywhere, vmem(), anywhere),
         out_shape=(
             jax.ShapeDtypeStruct(part.shape, jnp.float32),
             jax.ShapeDtypeStruct(prev.shape, jnp.bfloat16),
             jax.ShapeDtypeStruct(grad.shape, jnp.bfloat16),
         ),
-        input_output_aliases={4: 0},
+        input_output_aliases={7: 0},
         scratch_shapes=[square] * 4
         + [
             pltpu.VMEM(grad.shape, jnp.bfloat16),
+            pltpu.VMEM((group - 1, B, order), jnp.bfloat16),
             pltpu.VMEM((2 * (group - 1), B, B), jnp.float32),
-            pltpu.SemaphoreType.DMA((2 * group,)),
+            pltpu.SemaphoreType.DMA((3 * group - 1,)),
         ],
         compiler_params=params(60),
         cost_estimate=cost(10 * order**3, 8 * MIB),
         name="root",
-    )(flags, pieces, prev, grad, part)
-
-
-def kept_kernel(
-    group, flags_ref, first_hbm, prev_hbm, second_hbm, third_hbm, grad_hbm, old_hbm, update_hbm, *scratch
-):
-    upper_ref, grad_ref, half_ref, whole_ref, new_ref, sems = scratch
-    me, live = flags_ref[0], flags_ref[1]
-    step = 2 * B
-
-    @pl.when(live == 0)
-    def _():
-        uppers = (prev_hbm.at[:B, :], first_hbm, second_hbm, third_hbm)
-        loads = [pltpu.make_async_copy(uppers[k], upper_ref.at[k], sems.at[k]) for k in range(group)]
-        loads.append(pltpu.make_async_copy(old_hbm.at[: group * B, :], half_ref, sems.at[group]))
-        loads.append(pltpu.make_async_copy(grad_hbm, grad_ref, sems.at[group + 1]))
-        for load in loads:
-            load.start()
-        for k in range(group):
-            loads[k].wait()
-            source = lax.rem(me - k + group, group)
-            whole_ref[pl.ds(pl.multiple_of(source * step, step), B), :] = upper_ref[k]
-        loads[group].wait()
-        for s in range(group):
-            whole_ref[s * step + B : (s + 1) * step, :] = half_ref[s * B : (s + 1) * B, :]
-        loads[group + 1].wait()
-
-        def line(i, _):
-            here = pl.ds(pl.multiple_of(i * step, step), step)
-            new_ref[here, :] = dot(grad_ref[here, :], whole_ref[...]).astype(jnp.bfloat16)
-            pltpu.make_async_copy(new_ref.at[here, :], update_hbm.at[here, :], sems.at[group + 2]).start()
-            return 0
-
-        lax.fori_loop(0, grad_ref.shape[0] // step, line, 0)
-        pltpu.make_async_copy(new_ref, update_hbm, sems.at[group + 2]).wait()
-
-
-def kept_update(flags, first, prev, second, third, grad, update):
-    group = 4
-    wide, order = grad.shape
-    anywhere = pl.BlockSpec(memory_space=pl.ANY)
-    return pl.pallas_call(
-        functools.partial(kept_kernel, group),
-        in_specs=[smem()] + [anywhere] * 6,
-        out_specs=anywhere,
-        out_shape=jax.ShapeDtypeStruct(grad.shape, jnp.bfloat16),
-        input_output_aliases={6: 0},
-        scratch_shapes=[
-            pltpu.VMEM((group, B, order), jnp.bfloat16),
-            pltpu.VMEM(grad.shape, jnp.bfloat16),
-            pltpu.VMEM((group * B, order), jnp.bfloat16),
-            pltpu.VMEM((order, order), jnp.bfloat16),
-            pltpu.VMEM(grad.shape, jnp.bfloat16),
-            pltpu.SemaphoreType.DMA((group + 3,)),
-        ],
-        compiler_params=params(60),
-        cost_estimate=cost(2 * wide * order * order, 8 * MIB),
-        name="kept",
-    )(flags, first, prev, second, third, grad, update)
+    )(flags, pieces, prev, *uppers, grad, part)
 
 
 def step_of(tokens, cotangent, routing, stat_prev, root_prev, owner_map):
@@ -513,19 +467,16 @@
 
     prev = root_prev[0]
     upper = prev[:B]
-    from_1 = shifted(upper, 1)
-    from_3 = shifted(upper, 3)
+    uppers = [shifted(upper, k) for k in range(1, group)]
     sent = dispatch(routing.reshape(1, rows), tokens, cotangent, experts)
     sent = sent.reshape(experts, SLOTS, wide + order)
     got = lax.all_to_all(sent, "expert", 0, 0, tiled=True)
     grad, part = gradient(got.reshape(experts * SLOTS, -1), group, wide, 1.0 / math.sqrt(rows))
     parts = lax.all_to_all(part, "group", 0, 0, tiled=True)
+    parts, *uppers = lax.optimization_barrier((parts, *uppers))
     stat_own, send = new_statistic(flags, parts, stat_prev[0], prev, wide * group)
     pieces = lax.all_to_all(send, "group", 0, 0, tiled=True)
-    pieces, upper = lax.optimization_barrier((pieces, upper))
-    from_2 = shifted(upper, 2)
-    stat, root_rows, update = inverse_root(flags, pieces, prev, grad, stat_own)
-    update = kept_update(flags, from_1, prev, from_2, from_3, grad, update)
+    stat, root_rows, update = inverse_root(flags, pieces, prev, uppers, grad, stat_own)
     return stat[None], root_rows[None], update[None]
 
 

time: 230 us -> 238 us (1.035)
  the two profiles are of different devices: /device:TPU:32 before, /device:TPU:9 now
where the time goes in v4:
time: 238 us; the launch traced here: 237 us
  blocking collectives  153 us (64%)
  waiting for transfers between devices  39.5 us (17%)
  Pallas kernels  34.7 us (15%)
  starting transfers between devices  8.43 us (4%)
    all_to_all x1, blocking collectives, step_of(): got = lax.all_to_all(sent, 'expert', 0, 0, tiled=True)  114 us
    ppermute x3, waiting for transfers between devices, shifted(): lax.ppermute(x, 'group', [(g, (g + k) % group) for g in range(group)])  39.5 us
    all_to_all x1, blocking collectives, step_of(): pieces = lax.all_to_all(send, 'group', 0, 0, tiled=True)  38.7 us
    pallas_call x1, Pallas kernels, inverse_root(): pl.pallas_call(functools.partial(root_kernel, group), in_specs=[smem(), v...  20.1 us
    pallas_call x1, Pallas kernels, gradient(): pl.pallas_call(functools.partial(gradient_kernel, group, scale), in_specs...  7.04 us
    pallas_call x1, Pallas kernels, dispatch(): pl.pallas_call(functools.partial(dispatch_kernel, experts), grid=(total /...  5.69 us
  transfers between devices with their start and end apart: 4, of which 2 were waited for; matrix products, arithmetic and copies ran while one was open for 0% of the time, Pallas kernels for 0%

profile of v4, /device:TPU:9, one launch (start us, length us, event | category | flops | bytes accessed | tf_op | source)
XLA Modules:
  0.0 237.4 jit_solution(4269424512246361832)
XLA Ops:
  0.6 5.7 %dispatch.1 = bf16[1024,2048]{1,0:T(8,128)(2,1)} custom-call(s32[1,480]{1,0:T(1,128)} %bitcast.18, bf16[480,1024]{1,0:T(8,128)(2,1)} %tok_hbm.1, bf16[480,1024]{1,0:T(8,128)(2,1)} %sig_hbm.1), custom_call_target="tpu_custom_call" | custom-call | flops 2013265920 | bytes 6291456 | tf_op jit(solution)/shard_map/dispatch/pallas_call | solution.py:86
  6.3 113.9 %all_to_all.15 = bf16[64,16,2048]{2,1,0:T(8,128)(2,1)} all-to-all(bf16[64,16,2048]{2,1,0:T(8,128)(2,1)} %bitcast.16), channel_id=1, replica_groups=mesh['expert'=64,'group'=4] {'expert'}, dimensions={0} | all-to-all | bytes 8388608 | tf_op jit(solution)/shard_map/all_to_all | solution.py:473
  120.2 7.0 %gradient.1 = (bf16[1024,1024]{1,0:T(8,128)(2,1)}, bf16[4,1152,128]{2,1,0:T(8,128)(2,1)}) custom-call(bf16[1024,2048]{1,0:T(8,128)(2,1)} %bitcast.15), custom_call_target="tpu_custom_call" | custom-call | flops 4294967296 | bytes 10485760 | tf_op jit(solution)/shard_map/gradient/pallas_call | solution.py:163
  127.3 0.0 copy-start
  127.3 0.0 copy-start.5
  127.3 0.0 copy-start.1
  127.3 3.7 %all-to-all-start.1 = ((bf16[4,1152,128]{2,1,0:T(8,128)(2,1)}), bf16[4,1152,128]{2,1,0:T(8,128)(2,1)S(1)}, u32[]{:S(2)}, u32[]{:S(2)}) async-start(bf16[4,1152,128]{2,1,0:T(8,128)(2,1)} %get-tuple-element.14), calls=%async_computation.1 | async-start | bytes 2359296 | tf_op jit(solution)/shard_map/all_to_all | solution.py:475
  131.0 0.0 copy-done
  131.0 1.5 collective-permute-start
  132.5 2.1 collective-permute-start.1
  134.6 1.2 collective-permute-start.2
  135.8 0.0 copy-done.5
  135.8 0.6 dynamic-slice.2
  137.0 0.1 pad_add_fusion.flags_ref
  137.1 0.0 copy-start.2
  137.1 23.0 %collective-permute-done.first_hbm = bf16[128,1024]{1,0:T(8,128)(2,1)S(1)} collective-permute-done((bf16[128,1024]{1,0:T(8,128)(2,1)S(1)}, bf16[128,1024]{1,0:T(8,128)(2,1)S(1)}, u32[]{:S(2)}, u32[]{:S(2)}) %collective-permute-start) | collective-permute-done | bytes 262176 | tf_op jit(solution)/shard_map/ppermute | solution.py:466
  160.1 0.0 copy-start.3
  160.1 16.5 %collective-permute-done.1.second_hbm = bf16[128,1024]{1,0:T(8,128)(2,1)S(1)} collective-permute-done((bf16[128,1024]{1,0:T(8,128)(2,1)S(1)}, bf16[128,1024]{1,0:T(8,128)(2,1)S(1)}, u32[]{:S(2)}, u32[]{:S(2)}) %collective-permute-start.1) | collective-permute-done | bytes 262176 | tf_op jit(solution)/shard_map/ppermute | solution.py:466
  176.6 0.0 copy-start.4
  176.6 0.0 collective-permute-done.2.third_hbm
  176.6 0.0 all-to-all-done.1.parts_ref
  176.6 0.0 copy-done.1
  176.6 1.9 statistic.1
  178.5 38.7 %all_to_all.16.pieces_ref = bf16[4,1280,128]{2,1,0:T(8,128)(2,1)} all-to-all(bf16[4,1280,128]{2,1,0:T(8,128)(2,1)S(1)} %get-tuple-element.16), channel_id=1, replica_groups=mesh['expert'=64,'group'=4] {'group'}, dimensions={0} | all-to-all | bytes 2621440 | tf_op jit(solution)/shard_map/all_to_all | solution.py:478
  217.3 0.0 copy-done.2
  217.3 0.0 copy-done.3
  217.3 0.0 copy-done.4
  217.3 20.1 %root.1 = (f32[256,1024]{1,0:T(8,128)}, bf16[256,1024]{1,0:T(8,128)(2,1)}, bf16[1024,1024]{1,0:T(8,128)(2,1)}) custom-call(s32[2]{0:T(128)} %copy-done.2, bf16[4,1280,128]{2,1,0:T(8,128)(2,1)} %all_to_all.16.pieces_ref, bf16[256,1024]{1,0:T(8,128)(2,1)} %bitcast.12, bf16[128,1024]{1,0:T(8,128)(2,1)} %copy-done.3, ...), custom_call_target="tpu_custom_call", output_to_operand_aliasing={{0}: (7, {})} | custom-call | flops 10737418240 | bytes 8388608 | tf_op jit(solution)/shard_map/root/pallas_call | solution.py:431
  (1 shorter events, 0.0 us)
Async XLA Ops:
  127.3 3.7 %copy-start = (bf16[1,256,1024]{2,1,0:T(8,128)(2,1)S(1)}, bf16[1,256,1024]{2,1,0:T(8,128)(2,1)}, u32[]{:S(2)}) copy-start(bf16[1,256,1024]{2,1,0:T(8,128)(2,1)} %param.10) | copy-start | bytes 1572868
  127.3 8.5 %copy-start.5 = (s32[64]{0:T(128)S(1)}, s32[64]{0:T(128)}, u32[]{:S(2)}) copy-start(s32[64]{0:T(128)} %param.11) | copy-start | bytes 772
  127.3 49.3 %copy-start.1 = (f32[1,256,1024]{2,1,0:T(8,128)S(1)}, f32[1,256,1024]{2,1,0:T(8,128)}, u32[]{:S(2)}) copy-start(f32[1,256,1024]{2,1,0:T(8,128)} %param.9) | copy-start | bytes 3145732
  127.3 49.3 %all-to-all-start.1 = ((bf16[4,1152,128]{2,1,0:T(8,128)(2,1)}), bf16[4,1152,128]{2,1,0:T(8,128)(2,1)S(1)}, u32[]{:S(2)}, u32[]{:S(2)}) async-start(bf16[4,1152,128]{2,1,0:T(8,128)(2,1)} %get-tuple-element.14), calls=%async_computation.1 | async-start | bytes 2359296 | tf_op jit(solution)/shard_map/all_to_all | solution.py:475
  131.0 29.1 %collective-permute-start = (bf16[128,1024]{1,0:T(8,128)(2,1)S(1)}, bf16[128,1024]{1,0:T(8,128)(2,1)S(1)}, u32[]{:S(2)}, u32[]{:S(2)}) collective-permute-start(bf16[128,1024]{1,0:T(8,128)(2,1)S(1)} %slice_bitcast_fusion), channel_id=1, source_target_pairs={{0,1},{1,2},{2,3},{3,0},{4,5},{5,6},{6,7},{7,4},{8,9},{9,10},{10,1... | collective-permute-start | bytes 786440 | tf_op jit(solution)/shard_map/ppermute | solution.py:466
  132.5 44.1 %collective-permute-start.1 = (bf16[128,1024]{1,0:T(8,128)(2,1)S(1)}, bf16[128,1024]{1,0:T(8,128)(2,1)S(1)}, u32[]{:S(2)}, u32[]{:S(2)}) collective-permute-start(bf16[128,1024]{1,0:T(8,128)(2,1)S(1)} %slice_bitcast_fusion), channel_id=1, source_target_pairs={{0,2},{1,3},{2,0},{3,1},{4,6},{5,7},{6,4},{7,5},{8,10},{9,11},{10,... | collective-permute-start | bytes 786440 | tf_op jit(solution)/shard_map/ppermute | solution.py:466
  134.6 42.0 %collective-permute-start.2 = (bf16[128,1024]{1,0:T(8,128)(2,1)S(1)}, bf16[128,1024]{1,0:T(8,128)(2,1)}, u32[]{:S(2)}, u32[]{:S(2)}) collective-permute-start(bf16[128,1024]{1,0:T(8,128)(2,1)S(1)} %slice_bitcast_fusion), channel_id=1, source_target_pairs={{0,3},{1,0},{2,1},{3,2},{4,7},{5,4},{6,5},{7,6},{8,11},{9,8},{10,9... | collective-permute-start | bytes 786440 | tf_op jit(solution)/shard_map/ppermute | solution.py:466
  137.1 80.1 %copy-start.2 = (s32[2]{0:T(128)}, s32[2]{0:T(128)S(1)}, u32[]{:S(2)}) copy-start(s32[2]{0:T(128)S(1)} %pad_add_fusion.flags_ref) | copy-start | bytes 28
  160.1 57.2 %copy-start.3 = (bf16[128,1024]{1,0:T(8,128)(2,1)}, bf16[128,1024]{1,0:T(8,128)(2,1)S(1)}, u32[]{:S(2)}) copy-start(bf16[128,1024]{1,0:T(8,128)(2,1)S(1)} %collective-permute-done.first_hbm) | copy-start | bytes 786436
  176.6 40.6 %copy-start.4 = (bf16[128,1024]{1,0:T(8,128)(2,1)}, bf16[128,1024]{1,0:T(8,128)(2,1)S(1)}, u32[]{:S(2)}) copy-start(bf16[128,1024]{1,0:T(8,128)(2,1)S(1)} %collective-permute-done.1.second_hbm) | copy-start | bytes 786436

commit v5 on v4

--- a/solution.py
+++ b/solution.py
@@ -82,7 +82,7 @@
 def dispatch(route, tokens, signal, experts):
     count, wide = tokens.shape
     hidden = signal.shape[1]
-    total, rows = experts * SLOTS, 2 * B
+    total, rows = experts * SLOTS, B
     return pl.pallas_call(
         functools.partial(dispatch_kernel, experts),
         grid=(total // rows,),
@@ -112,24 +112,16 @@
     return found
 
 
-def gradient_kernel(group, scale, x_hbm, grad_hbm, part_hbm, x_ref, grad_ref, part_ref, sems):
+def gradient_kernel(group, scale, x_ref, grad_hbm, part_hbm, grad_ref, part_ref, sems):
     wide = grad_ref.shape[0]
     step = 2 * B
     lines = wide // step
-    loads = [pltpu.make_async_copy(x_hbm.at[:, wide:], x_ref.at[:, wide:], sems.at[0])]
     stores = []
     for r in range(lines):
         at = slice(r * step, (r + 1) * step)
-        loads.append(pltpu.make_async_copy(x_hbm.at[:, at], x_ref.at[:, at], sems.at[1 + r]))
-        stores.append(pltpu.make_async_copy(grad_ref.at[at, :], grad_hbm.at[at, :], sems.at[1 + lines + r]))
-    for load in loads:
-        load.start()
-    loads[0].wait()
-    for r in range(lines):
-        loads[1 + r].wait()
-        at = slice(r * step, (r + 1) * step)
         grad_ref[at, :] = (outer(x_ref[:, at], x_ref[:, wide:]) * scale).astype(jnp.bfloat16)
-        stores[r].start()
+        stores.append(pltpu.make_async_copy(grad_ref.at[at, :], grad_hbm.at[at, :], sems.at[r]))
+        stores[-1].start()
     place = {}
     for d in range(group):
         for k, name in enumerate(owned_blocks(d, group)):
@@ -149,8 +141,7 @@
                         ]
             for d in range(group):
                 if last[d] == (p, q):
-                    sem = sems.at[1 + 2 * lines + d]
-                    stores.append(pltpu.make_async_copy(part_ref.at[d], part_hbm.at[d], sem))
+                    stores.append(pltpu.make_async_copy(part_ref.at[d], part_hbm.at[d], sems.at[lines + d]))
                     stores[-1].start()
     for store in stores:
         store.wait()
@@ -162,19 +153,18 @@
     part = (group, PIECE * B, B)
     return pl.pallas_call(
         functools.partial(gradient_kernel, group, scale),
-        in_specs=[pl.BlockSpec(memory_space=pl.ANY)],
+        in_specs=[vmem()],
         out_specs=(pl.BlockSpec(memory_space=pl.ANY),) * 2,
         out_shape=(
             jax.ShapeDtypeStruct((wide, hidden), jnp.bfloat16),
             jax.ShapeDtypeStruct(part, jnp.bfloat16),
         ),
         scratch_shapes=[
-            pltpu.VMEM(x.shape, jnp.bfloat16),
             pltpu.VMEM((wide, hidden), jnp.bfloat16),
             pltpu.VMEM(part, jnp.bfloat16),
-            pltpu.SemaphoreType.DMA((1 + 2 * (wide // (2 * B)) + group,)),
+            pltpu.SemaphoreType.DMA((wide // (2 * B) + group,)),
         ],
-        compiler_params=params(60),
+        compiler_params=params(16),
         cost_estimate=cost(2 * wide * hidden * (total + hidden), 10 * MIB),
         name="gradient",
     )(x)
@@ -266,20 +256,19 @@
     flags_ref,
     pieces_ref,
     prev_ref,
-    first_hbm,
-    second_hbm,
-    third_hbm,
+    first_ref,
+    second_ref,
+    third_ref,
     grad_hbm,
     part_hbm,
     stat_hbm,
-    rows_ref,
+    rows_hbm,
     update_hbm,
     a_ref,
     f_ref,
     g_ref,
     h_ref,
     grad_ref,
-    upper_ref,
     mirror_ref,
     sems,
 ):
@@ -288,16 +277,8 @@
     step = 2 * B
     done = sems.at[2 * group - 2]
     load = pltpu.make_async_copy(grad_hbm, grad_ref, sems.at[2 * group - 1])
-    uppers = [
-        pltpu.make_async_copy(source, upper_ref.at[k], sems.at[2 * group + k])
-        for k, source in enumerate((first_hbm, second_hbm, third_hbm))
-    ]
+    rows_sem = sems.at[2 * group]
     load.start()
-
-    @pl.when(live == 0)
-    def _():
-        for upper in uppers:
-            upper.start()
 
     def mirrored(j):
         s = jnp.where(j < me, j, j + 1)
@@ -324,16 +305,15 @@
 
     @pl.when(live == 0)
     def _():
-        rows_ref[...] = prev_ref[...]
+        pltpu.make_async_copy(prev_ref, rows_hbm, rows_sem).start()
         for s in range(group):
             for c in range(HALF):
                 g_ref[s * step + B : (s + 1) * step, c * B : (c + 1) * B] = pieces_ref[
                     s, (2 + c) * B : (3 + c) * B, :
                 ]
         g_ref[rows_of(me, B), :] = prev_ref[:B, :]
-        for k in range(1, group):
-            uppers[k - 1].wait()
-            g_ref[rows_of(lax.rem(me - k + group, group), B), :] = upper_ref[k - 1]
+        for k, upper_ref in enumerate((first_ref, second_ref, third_ref)):
+            g_ref[rows_of(lax.rem(me - k - 1 + group, group), B), :] = upper_ref[...]
 
     @pl.when(live != 0)
     def _():
@@ -406,7 +386,7 @@
             return 0
 
         lax.fori_loop(0, order // step, last, 0)
-        rows_ref[...] = g_ref[rows_of(me), :]
+        pltpu.make_async_copy(g_ref.at[rows_of(me), :], rows_hbm, rows_sem).start()
 
     load.wait()
 
@@ -418,6 +398,7 @@
 
     lax.fori_loop(0, order // step, line, 0)
     pltpu.make_async_copy(f_ref, update_hbm, done).wait()
+    pltpu.make_async_copy(prev_ref, rows_hbm, rows_sem).wait()
 
     for store in stores:
         store.wait()
@@ -430,22 +411,21 @@
     anywhere = pl.BlockSpec(memory_space=pl.ANY)
     return pl.pallas_call(
         functools.partial(root_kernel, group),
-        in_specs=[smem(), vmem(), vmem()] + [anywhere] * 5,
-        out_specs=(anywhere, vmem(), anywhere),
+        in_specs=[smem()] + [vmem()] * (1 + group) + [anywhere] * 2,
+        out_specs=(anywhere, anywhere, anywhere),
         out_shape=(
             jax.ShapeDtypeStruct(part.shape, jnp.float32),
             jax.ShapeDtypeStruct(prev.shape, jnp.bfloat16),
             jax.ShapeDtypeStruct(grad.shape, jnp.bfloat16),
         ),
-        input_output_aliases={7: 0},
+        input_output_aliases={7: 0, 6: 2},
         scratch_shapes=[square] * 4
         + [
             pltpu.VMEM(grad.shape, jnp.bfloat16),
-            pltpu.VMEM((group - 1, B, order), jnp.bfloat16),
             pltpu.VMEM((2 * (group - 1), B, B), jnp.float32),
-            pltpu.SemaphoreType.DMA((3 * group - 1,)),
+            pltpu.SemaphoreType.DMA((2 * group + 1,)),
         ],
-        compiler_params=params(60),
+        compiler_params=params(20),
         cost_estimate=cost(10 * order**3, 8 * MIB),
         name="root",
     )(flags, pieces, prev, *uppers, grad, part)

time: 238 us -> 235 us (0.987)
  Pallas kernels: 34.7 us -> 32.1 us
  transfers between devices with their start and end apart: 4 -> 4, of which waited for: 2 -> 2; matrix products, arithmetic and copies ran while one was open for 0% -> 1% of each run, Pallas kernels for 0% -> 0%
where the time goes in v5:
time: 235 us
  blocking collectives  152 us (65%)
  waiting for transfers between devices  39 us (17%)
  Pallas kernels  32.1 us (14%)
  starting transfers between devices  8.35 us (4%)
    all_to_all x1, blocking collectives, step_of(): got = lax.all_to_all(sent, 'expert', 0, 0, tiled=True)  114 us
    ppermute x3, waiting for transfers between devices, shifted(): lax.ppermute(x, 'group', [(g, (g + k) % group) for g in range(group)])  38.9 us
    all_to_all x1, blocking collectives, step_of(): pieces = lax.all_to_all(send, 'group', 0, 0, tiled=True)  38.6 us
    pallas_call x1, Pallas kernels, inverse_root(): pl.pallas_call(functools.partial(root_kernel, group), in_specs=[smem()] +...  18.4 us
    pallas_call x1, Pallas kernels, dispatch(): pl.pallas_call(functools.partial(dispatch_kernel, experts), grid=(total /...  7.01 us
    pallas_call x1, Pallas kernels, gradient(): pl.pallas_call(functools.partial(gradient_kernel, group, scale), in_specs...  4.87 us
  transfers between devices with their start and end apart: 4, of which 2 were waited for; matrix products, arithmetic and copies ran while one was open for 1% of the time, Pallas kernels for 0%

profile of v5, /device:TPU:9, one launch (start us, length us, event | category | flops | bytes accessed | tf_op | source)
XLA Modules:
  0.0 234.5 jit_solution(231016003871546504)
XLA Ops:
  0.6 7.0 %dispatch.1 = bf16[1024,2048]{1,0:T(8,128)(2,1)} custom-call(s32[1,480]{1,0:T(1,128)} %bitcast.18, bf16[480,1024]{1,0:T(8,128)(2,1)} %tok_hbm.1, bf16[480,1024]{1,0:T(8,128)(2,1)} %sig_hbm.1), custom_call_target="tpu_custom_call" | custom-call | flops 2013265920 | bytes 6291456 | tf_op jit(solution)/shard_map/dispatch/pallas_call | solution.py:86
  7.7 113.8 %all_to_all.15 = bf16[64,16,2048]{2,1,0:T(8,128)(2,1)S(1)} all-to-all(bf16[64,16,2048]{2,1,0:T(8,128)(2,1)} %bitcast.16), channel_id=1, replica_groups=mesh['expert'=64,'group'=4] {'expert'}, dimensions={0} | all-to-all | bytes 8388608 | tf_op jit(solution)/shard_map/all_to_all | solution.py:453
  121.4 4.9 %gradient.1 = (bf16[1024,1024]{1,0:T(8,128)(2,1)}, bf16[4,1152,128]{2,1,0:T(8,128)(2,1)}) custom-call(bf16[1024,2048]{1,0:T(8,128)(2,1)S(1)} %bitcast.12), custom_call_target="tpu_custom_call" | custom-call | flops 4294967296 | bytes 10485760 | tf_op jit(solution)/shard_map/gradient/pallas_call | solution.py:154
  126.3 0.0 copy-start
  126.3 0.0 copy-start.2
  126.3 0.0 copy-start.1
  126.4 3.7 %all-to-all-start.1 = ((bf16[4,1152,128]{2,1,0:T(8,128)(2,1)}), bf16[4,1152,128]{2,1,0:T(8,128)(2,1)S(1)}, u32[]{:S(2)}, u32[]{:S(2)}) async-start(bf16[4,1152,128]{2,1,0:T(8,128)(2,1)} %get-tuple-element.14), calls=%async_computation.1 | async-start | bytes 2359296 | tf_op jit(solution)/shard_map/all_to_all | solution.py:455
  130.0 0.0 copy-done
  130.0 0.7 slice_bitcast_fusion
  130.8 1.4 collective-permute-start
  132.2 2.1 collective-permute-start.1
  134.3 1.2 collective-permute-start.2
  135.4 0.0 copy-done.2
  135.4 0.6 dynamic-slice.2
  136.6 0.1 pad_add_fusion.flags_ref
  136.7 22.4 %collective-permute-done.first_ref = bf16[128,1024]{1,0:T(8,128)(2,1)S(1)} collective-permute-done((bf16[128,1024]{1,0:T(8,128)(2,1)}, bf16[128,1024]{1,0:T(8,128)(2,1)S(1)}, u32[]{:S(2)}, u32[]{:S(2)}) %collective-permute-start) | collective-permute-done | bytes 262176 | tf_op jit(solution)/shard_map/ppermute | solution.py:446
  159.1 16.5 %collective-permute-done.1.second_ref = bf16[128,1024]{1,0:T(8,128)(2,1)S(1)} collective-permute-done((bf16[128,1024]{1,0:T(8,128)(2,1)}, bf16[128,1024]{1,0:T(8,128)(2,1)S(1)}, u32[]{:S(2)}, u32[]{:S(2)}) %collective-permute-start.1) | collective-permute-done | bytes 262176 | tf_op jit(solution)/shard_map/ppermute | solution.py:446
  175.6 0.0 collective-permute-done.2.third_ref
  175.6 0.0 all-to-all-done.1.parts_ref
  175.7 0.0 copy-done.1
  175.7 1.9 statistic.1
  177.5 38.6 %all_to_all.16.pieces_ref = bf16[4,1280,128]{2,1,0:T(8,128)(2,1)S(1)} all-to-all(bf16[4,1280,128]{2,1,0:T(8,128)(2,1)S(1)} %get-tuple-element.16), channel_id=1, replica_groups=mesh['expert'=64,'group'=4] {'group'}, dimensions={0} | all-to-all | bytes 2621440 | tf_op jit(solution)/shard_map/all_to_all | solution.py:458
  216.1 18.4 %root.1 = (f32[256,1024]{1,0:T(8,128)}, bf16[256,1024]{1,0:T(8,128)(2,1)}, bf16[1024,1024]{1,0:T(8,128)(2,1)}) custom-call(s32[2]{0:T(128)S(1)} %pad_add_fusion.flags_ref, bf16[4,1280,128]{2,1,0:T(8,128)(2,1)S(1)} %all_to_all.16.pieces_ref, bf16[256,1024]{1,0:T(8,128)(2,1)S(1)} %bitcast.14, ...), custom_call_target="tpu_custom_call", output_to_operand_aliasing={{0}: (7, {}), {2}: (6, {})} | custom-call | flops 10737418240 | bytes 8388608 | tf_op jit(solution)/shard_map/root/pallas_call | solution.py:412
Async XLA Ops:
  126.3 3.7 %copy-start = (bf16[1,256,1024]{2,1,0:T(8,128)(2,1)S(1)}, bf16[1,256,1024]{2,1,0:T(8,128)(2,1)}, u32[]{:S(2)}) copy-start(bf16[1,256,1024]{2,1,0:T(8,128)(2,1)} %param.10) | copy-start | bytes 1572868
  126.3 9.1 %copy-start.2 = (s32[64]{0:T(128)S(1)}, s32[64]{0:T(128)}, u32[]{:S(2)}) copy-start(s32[64]{0:T(128)} %param.11) | copy-start | bytes 772
  126.3 49.3 %copy-start.1 = (f32[1,256,1024]{2,1,0:T(8,128)S(1)}, f32[1,256,1024]{2,1,0:T(8,128)}, u32[]{:S(2)}) copy-start(f32[1,256,1024]{2,1,0:T(8,128)} %param.9) | copy-start | bytes 3145732
  126.4 49.3 %all-to-all-start.1 = ((bf16[4,1152,128]{2,1,0:T(8,128)(2,1)}), bf16[4,1152,128]{2,1,0:T(8,128)(2,1)S(1)}, u32[]{:S(2)}, u32[]{:S(2)}) async-start(bf16[4,1152,128]{2,1,0:T(8,128)(2,1)} %get-tuple-element.14), calls=%async_computation.1 | async-start | bytes 2359296 | tf_op jit(solution)/shard_map/all_to_all | solution.py:455
  130.8 28.4 %collective-permute-start = (bf16[128,1024]{1,0:T(8,128)(2,1)}, bf16[128,1024]{1,0:T(8,128)(2,1)S(1)}, u32[]{:S(2)}, u32[]{:S(2)}) collective-permute-start(bf16[128,1024]{1,0:T(8,128)(2,1)} %slice_bitcast_fusion), channel_id=1, source_target_pairs={{0,1},{1,2},{2,3},{3,0},{4,5},{5,6},{6,7},{7,4},{8,9},{9,10},{10,1... | collective-permute-start | bytes 786440 | tf_op jit(solution)/shard_map/ppermute | solution.py:446
  132.2 43.5 %collective-permute-start.1 = (bf16[128,1024]{1,0:T(8,128)(2,1)}, bf16[128,1024]{1,0:T(8,128)(2,1)S(1)}, u32[]{:S(2)}, u32[]{:S(2)}) collective-permute-start(bf16[128,1024]{1,0:T(8,128)(2,1)} %slice_bitcast_fusion), channel_id=1, source_target_pairs={{0,2},{1,3},{2,0},{3,1},{4,6},{5,7},{6,4},{7,5},{8,10},{9,11},{10,... | collective-permute-start | bytes 786440 | tf_op jit(solution)/shard_map/ppermute | solution.py:446
  134.3 41.4 %collective-permute-start.2 = (bf16[128,1024]{1,0:T(8,128)(2,1)}, bf16[128,1024]{1,0:T(8,128)(2,1)S(1)}, u32[]{:S(2)}, u32[]{:S(2)}) collective-permute-start(bf16[128,1024]{1,0:T(8,128)(2,1)} %slice_bitcast_fusion), channel_id=1, source_target_pairs={{0,3},{1,0},{2,1},{3,2},{4,7},{5,4},{6,5},{7,6},{8,11},{9,8},{10,9... | collective-permute-start | bytes 786440 | tf_op jit(solution)/shard_map/ppermute | solution.py:446

commit v6 on v5

--- a/solution.py
+++ b/solution.py
@@ -13,8 +13,8 @@
 KEEP = 0.9
 SLOTS = 16
 B = 128
-HALF = 8
 PIECE = 9
+REST = 112
 MIB = 1024 * 1024
 
 
@@ -46,55 +46,57 @@
     return jnp.where(mask, 1.0, 0.0).astype(jnp.bfloat16)
 
 
-def dispatch_kernel(experts, route_hbm, tok_hbm, sig_hbm, out_ref, route_ref, slot_ref, tok_ref, sig_ref, sems):
+def dispatch_kernel(experts, route_hbm, tok_hbm, sig_hbm, out_hbm, route_ref, tok_ref, sig_ref, out_ref, sems):
     tokens = route_ref.shape[1]
     wide = tok_ref.shape[1]
-    rows = out_ref.shape[0]
-
-    @pl.when(pl.program_id(0) == 0)
-    def _():
-        copies = [
-            pltpu.make_async_copy(route_hbm, route_ref, sems.at[0]),
-            pltpu.make_async_copy(tok_hbm, tok_ref, sems.at[1]),
-            pltpu.make_async_copy(sig_hbm, sig_ref, sems.at[2]),
-        ]
-        for copy in copies:
-            copy.start()
-        before = lax.broadcasted_iota(jnp.int32, (tokens, tokens), 0) < lax.broadcasted_iota(
-            jnp.int32, (tokens, tokens), 1
-        )
-        before = ones_where(before)
-        copies[0].wait()
-        route = route_ref[...]
-        hot = lax.broadcasted_iota(jnp.int32, (experts, tokens), 0) == route
-        earlier = dot(ones_where(hot), before)
-        position = jnp.sum(jnp.where(hot, earlier, 0.0), axis=0, keepdims=True)
-        slot_ref[...] = route * SLOTS + position.astype(jnp.int32)
-        copies[1].wait()
-        copies[2].wait()
-
-    at = lax.broadcasted_iota(jnp.int32, (rows, tokens), 0) + pl.program_id(0) * rows
-    pick = ones_where(at == slot_ref[...])
-    out_ref[:, :wide] = dot(pick, tok_ref[...]).astype(jnp.bfloat16)
-    out_ref[:, wide:] = dot(pick, sig_ref[...]).astype(jnp.bfloat16)
+    rows = 2 * B
+    loads = [
+        pltpu.make_async_copy(route_hbm, route_ref, sems.at[0]),
+        pltpu.make_async_copy(tok_hbm, tok_ref, sems.at[1]),
+        pltpu.make_async_copy(sig_hbm, sig_ref, sems.at[2]),
+    ]
+    for load in loads:
+        load.start()
+    before = lax.broadcasted_iota(jnp.int32, (tokens, tokens), 0) < lax.broadcasted_iota(
+        jnp.int32, (tokens, tokens), 1
+    )
+    before = ones_where(before)
+    loads[0].wait()
+    route = route_ref[...]
+    hot = lax.broadcasted_iota(jnp.int32, (experts, tokens), 0) == route
+    earlier = dot(ones_where(hot), before)
+    position = jnp.sum(jnp.where(hot, earlier, 0.0), axis=0, keepdims=True)
+    slot = route * SLOTS + position.astype(jnp.int32)
+    line = lax.broadcasted_iota(jnp.int32, (rows, tokens), 0)
+    stores = []
+    for part, (source, col) in enumerate(((tok_ref, 0), (sig_ref, wide))):
+        loads[1 + part].wait()
+        for start in range(0, out_ref.shape[0], rows):
+            at = (slice(start, start + rows), slice(col, col + source.shape[1]))
+            pick = ones_where(line + start == slot)
+            out_ref[at] = dot(pick, source[...]).astype(jnp.bfloat16)
+            stores.append(pltpu.make_async_copy(out_ref.at[at], out_hbm.at[at], sems.at[3 + len(stores)]))
+            stores[-1].start()
+    for store in stores:
+        store.wait()
 
 
 def dispatch(route, tokens, signal, experts):
     count, wide = tokens.shape
     hidden = signal.shape[1]
-    total, rows = experts * SLOTS, B
+    total = experts * SLOTS
+    anywhere = pl.BlockSpec(memory_space=pl.ANY)
     return pl.pallas_call(
         functools.partial(dispatch_kernel, experts),
-        grid=(total // rows,),
-        in_specs=[pl.BlockSpec(memory_space=pl.ANY)] * 3,
-        out_specs=pl.BlockSpec((rows, wide + hidden), lambda i: (i, 0)),
+        in_specs=[anywhere] * 3,
+        out_specs=anywhere,
         out_shape=jax.ShapeDtypeStruct((total, wide + hidden), jnp.bfloat16),
         scratch_shapes=[
             pltpu.VMEM((1, count), jnp.int32),
-            pltpu.VMEM((1, count), jnp.int32),
             pltpu.VMEM((count, wide), jnp.bfloat16),
             pltpu.VMEM((count, hidden), jnp.bfloat16),
-            pltpu.SemaphoreType.DMA((3,)),
+            pltpu.VMEM((total, wide + hidden), jnp.bfloat16),
+            pltpu.SemaphoreType.DMA((3 + 2 * (total // (2 * B)),)),
         ],
         compiler_params=params(60),
         cost_estimate=cost(2 * total * count * (wide + hidden), 6 * MIB),
@@ -213,13 +215,14 @@
     @pl.when(live != 0)
     def _():
         for t in range(group):
-            send_ref[t, : PIECE * B, :] = own_ref[...]
+            send_ref[t] = own_ref[...]
 
     @pl.when(live == 0)
     def _():
         for t in range(group):
-            for c in range(HALF):
-                send_ref[t, (2 + c) * B : (3 + c) * B, :] = root_ref[B:, c * B : (c + 1) * B]
+            for c in range(root_ref.shape[1] // B):
+                at = slice(2 * B + c * REST, 2 * B + (c + 1) * REST)
+                send_ref[t, at, :] = root_ref[-REST:, c * B : (c + 1) * B]
             send_ref[t, : 2 * B, :] = own_ref[pl.ds(shared(me, t), 2 * B), :]
 
     store.wait()
@@ -238,7 +241,7 @@
         out_specs=(pl.BlockSpec(memory_space=pl.ANY), vmem()),
         out_shape=(
             jax.ShapeDtypeStruct(prev.shape, jnp.float32),
-            jax.ShapeDtypeStruct((group, (2 + HALF) * B, B), jnp.bfloat16),
+            jax.ShapeDtypeStruct((group, PIECE * B, B), jnp.bfloat16),
         ),
         scratch_shapes=[
             pltpu.VMEM(prev.shape, jnp.float32),
@@ -268,6 +271,7 @@
     f_ref,
     g_ref,
     h_ref,
+    s_ref,
     grad_ref,
     mirror_ref,
     sems,
@@ -307,13 +311,12 @@
     def _():
         pltpu.make_async_copy(prev_ref, rows_hbm, rows_sem).start()
         for s in range(group):
-            for c in range(HALF):
-                g_ref[s * step + B : (s + 1) * step, c * B : (c + 1) * B] = pieces_ref[
-                    s, (2 + c) * B : (3 + c) * B, :
-                ]
-        g_ref[rows_of(me, B), :] = prev_ref[:B, :]
+            for c in range(order // B):
+                at = slice(2 * B + c * REST, 2 * B + (c + 1) * REST)
+                g_ref[(s + 1) * step - REST : (s + 1) * step, c * B : (c + 1) * B] = pieces_ref[s, at, :]
+        g_ref[rows_of(me, step - REST), :] = prev_ref[: step - REST, :]
         for k, upper_ref in enumerate((first_ref, second_ref, third_ref)):
-            g_ref[rows_of(lax.rem(me - k - 1 + group, group), B), :] = upper_ref[...]
+            g_ref[rows_of(lax.rem(me - k - 1 + group, group), step - REST), :] = upper_ref[...]
 
     @pl.when(live != 0)
     def _():
@@ -339,53 +342,67 @@
                 if h != s:
                     k += 2
 
-        def power(_, carry):
-            vector, _ = carry
-            image = dot(vector.astype(jnp.bfloat16), a_ref[...])
+        lines = range(order // step)
+        row = lax.broadcasted_iota(jnp.int32, (step, step), 0)
+        eye = row == lax.broadcasted_iota(jnp.int32, (step, step), 1)
+
+        def both(ref, i, j, block):
+            ref[i * step : (i + 1) * step, j * step : (j + 1) * step] = block
+            if i != j:
+                ref[j * step : (j + 1) * step, i * step : (i + 1) * step] = block.T
+
+        def piece(ref, i, j):
+            return ref[i * step : (i + 1) * step, j * step : (j + 1) * step]
+
+        def upper_product(left, right, use):
+            for i in lines:
+                found = dot(left[i * step : (i + 1) * step, :], right[:, i * step :])
+                for j in lines[i:]:
+                    use(i, j, found[:, (j - i) * step : (j - i + 1) * step])
+
+        largest = jnp.zeros((1, step), jnp.float32)
+        for i in lines:
+            diagonal = jnp.where(eye, piece(a_ref, i, i).astype(jnp.float32), 0.0)
+            largest = jnp.maximum(largest, jnp.max(diagonal, axis=0, keepdims=True))
+        unit = 1.0 / jnp.max(largest, axis=1, keepdims=True)
+
+        def squared(i, j, block):
+            s_ref[i * step : (i + 1) * step, j * step : (j + 1) * step] = block
+            both(g_ref, i, j, (block * unit * unit).astype(jnp.bfloat16))
+
+        upper_product(a_ref, a_ref, squared)
+
+        def applied(vector, matrix_ref):
+            image = dot(vector.astype(jnp.bfloat16), matrix_ref[...])
             length = jnp.sqrt(jnp.sum(image * image, axis=1, keepdims=True))
             return image / length, length
 
         vector = jnp.full((16, order), 1.0 / math.sqrt(order), jnp.float32)
-        length = jnp.ones((16, 1), jnp.float32)
-        _, length = lax.fori_loop(0, POWER, power, (vector, length))
+        vector = lax.fori_loop(0, POWER // 2 - 1, lambda _, v: applied(v, g_ref)[0], vector)
+        vector, _ = applied(vector, a_ref)
+        _, length = applied(vector, a_ref)
         scaling = 2.5 / length[:1, :1]
         quarter = jnp.sqrt(jnp.sqrt(scaling)) * 0.25
 
-        def first(i, _):
-            here = rows_of(i)
-            line = lax.broadcasted_iota(jnp.int32, (step, order), 0) + i * step
-            eye = line == lax.broadcasted_iota(jnp.int32, (step, order), 1)
-            moment = scaling * a_ref[here, :].astype(jnp.float32)
-            f_ref[here, :] = ((jnp.where(eye, 5.0, 0.0) - moment) * 0.25).astype(jnp.bfloat16)
-            return 0
-
-        lax.fori_loop(0, order // step, first, 0)
-
-        def second(i, _):
-            here = rows_of(i)
-            factor = f_ref[here, :]
-            square = dot(factor, f_ref[...])
-            g_ref[here, :] = square.astype(jnp.bfloat16)
-            h_ref[here, :] = (5.0 * factor.astype(jnp.float32) - 4.0 * square).astype(jnp.bfloat16)
-            return 0
-
-        lax.fori_loop(0, order // step, second, 0)
-
-        def third(i, _):
-            here = rows_of(i)
-            a_ref[here, :] = dot(g_ref[here, :], g_ref[...]).astype(jnp.bfloat16)
-            return 0
-
-        lax.fori_loop(0, order // step, third, 0)
-
-        def last(i, _):
-            here = rows_of(i)
-            tail = dot(a_ref[here, :], h_ref[...])
-            factor = f_ref[here, :].astype(jnp.float32)
-            g_ref[here, :] = ((5.0 * factor - tail) * quarter).astype(jnp.bfloat16)
-            return 0
-
-        lax.fori_loop(0, order // step, last, 0)
+        for i in lines:
+            for j in lines[i:]:
+                moment = scaling * piece(a_ref, i, j).astype(jnp.float32)
+                twice = scaling * (scaling * piece(s_ref, i, j))
+                square = twice - 10.0 * moment
+                if i == j:
+                    square += jnp.where(eye, 25.0, 0.0)
+                both(g_ref, i, j, (square * 0.0625).astype(jnp.bfloat16))
+                both(h_ref, i, j, ((5.0 * moment - twice) * 0.25).astype(jnp.bfloat16))
+
+        upper_product(g_ref, g_ref, lambda i, j, block: both(f_ref, i, j, block.astype(jnp.bfloat16)))
+
+        def root(i, j, tail):
+            factor = -1.25 * scaling * piece(a_ref, i, j).astype(jnp.float32)
+            if i == j:
+                factor += jnp.where(eye, 6.25, 0.0)
+            both(g_ref, i, j, ((factor - tail) * quarter).astype(jnp.bfloat16))
+
+        upper_product(f_ref, h_ref, root)
         pltpu.make_async_copy(g_ref.at[rows_of(me), :], rows_hbm, rows_sem).start()
 
     load.wait()
@@ -421,11 +438,12 @@
         input_output_aliases={7: 0, 6: 2},
         scratch_shapes=[square] * 4
         + [
+            pltpu.VMEM((order, order), jnp.float32),
             pltpu.VMEM(grad.shape, jnp.bfloat16),
             pltpu.VMEM((2 * (group - 1), B, B), jnp.float32),
             pltpu.SemaphoreType.DMA((2 * group + 1,)),
         ],
-        compiler_params=params(20),
+        compiler_params=params(26),
         cost_estimate=cost(10 * order**3, 8 * MIB),
         name="root",
     )(flags, pieces, prev, *uppers, grad, part)
@@ -446,7 +464,7 @@
         return lax.ppermute(x, "group", [(g, (g + k) % group) for g in range(group)])
 
     prev = root_prev[0]
-    upper = prev[:B]
+    upper = prev[: prev.shape[0] - REST]
     uppers = [shifted(upper, k) for k in range(1, group)]
     sent = dispatch(routing.reshape(1, rows), tokens, cotangent, experts)
     sent = sent.reshape(experts, SLOTS, wide + order)

time: 235 us -> 227 us (0.966)
  Pallas kernels: 32.1 us -> 24.3 us
    pallas_call x1, Pallas kernels: 18.4 us -> 12.9 us  [inverse_root(): pl.pallas_call(functools.partial(root_kernel, group), in_specs=[smem()] +...]
    pallas_call x1, Pallas kernels: 7.01 us -> 4.65 us  [dispatch(): pl.pallas_call(functools.partial(dispatch_kernel, experts), in_specs=[any...]
where the time goes in v6:
time: 227 us
  blocking collectives  150 us (66%)
  waiting for transfers between devices  40.9 us (18%)
  Pallas kernels  24.3 us (11%)
  starting transfers between devices  8.35 us (4%)
    all_to_all x1, blocking collectives, step_of(): got = lax.all_to_all(sent, 'expert', 0, 0, tiled=True)  114 us
    ppermute x3, waiting for transfers between devices, shifted(): lax.ppermute(x, 'group', [(g, (g + k) % group) for g in range(group)])  40.9 us
    all_to_all x1, blocking collectives, step_of(): pieces = lax.all_to_all(send, 'group', 0, 0, tiled=True)  36.5 us
    pallas_call x1, Pallas kernels, inverse_root(): pl.pallas_call(functools.partial(root_kernel, group), in_specs=[smem()] +...  12.9 us
    pallas_call x1, Pallas kernels, gradient(): pl.pallas_call(functools.partial(gradient_kernel, group, scale), in_specs...  4.87 us
    ppermute x3, starting transfers between devices, shifted(): lax.ppermute(x, 'group', [(g, (g + k) % group) for g in range(group)])  4.68 us
    pallas_call x1, Pallas kernels, dispatch(): pl.pallas_call(functools.partial(dispatch_kernel, experts), in_specs=[any...  4.65 us
  transfers between devices with their start and end apart: 4, of which 2 were waited for; matrix products, arithmetic and copies ran while one was open for 1% of the time, Pallas kernels for 0%

profile of v6, /device:TPU:9, one launch (start us, length us, event | category | flops | bytes accessed | tf_op | source)
XLA Modules:
  0.0 226.9 jit_solution(9382396379380924684)
XLA Ops:
  0.6 4.6 %dispatch.1 = bf16[1024,2048]{1,0:T(8,128)(2,1)} custom-call(s32[1,480]{1,0:T(1,128)} %bitcast.18, bf16[480,1024]{1,0:T(8,128)(2,1)} %tok_hbm.1, bf16[480,1024]{1,0:T(8,128)(2,1)} %sig_hbm.1), custom_call_target="tpu_custom_call" | custom-call | flops 2013265920 | bytes 6291456 | tf_op jit(solution)/shard_map/dispatch/pallas_call | solution.py:89
  5.3 113.8 %all_to_all.15 = bf16[64,16,2048]{2,1,0:T(8,128)(2,1)S(1)} all-to-all(bf16[64,16,2048]{2,1,0:T(8,128)(2,1)} %bitcast.16), channel_id=1, replica_groups=mesh['expert'=64,'group'=4] {'expert'}, dimensions={0} | all-to-all | bytes 8388608 | tf_op jit(solution)/shard_map/all_to_all | solution.py:471
  119.1 4.9 %gradient.1 = (bf16[1024,1024]{1,0:T(8,128)(2,1)}, bf16[4,1152,128]{2,1,0:T(8,128)(2,1)}) custom-call(bf16[1024,2048]{1,0:T(8,128)(2,1)S(1)} %bitcast.12), custom_call_target="tpu_custom_call" | custom-call | flops 4294967296 | bytes 10485760 | tf_op jit(solution)/shard_map/gradient/pallas_call | solution.py:156
  124.0 0.0 copy-start
  124.0 0.0 copy-start.2
  124.0 0.0 copy-start.1
  124.0 3.7 %all-to-all-start.1 = ((bf16[4,1152,128]{2,1,0:T(8,128)(2,1)}), bf16[4,1152,128]{2,1,0:T(8,128)(2,1)S(1)}, u32[]{:S(2)}, u32[]{:S(2)}) async-start(bf16[4,1152,128]{2,1,0:T(8,128)(2,1)} %get-tuple-element.14), calls=%async_computation.1 | async-start | bytes 2359296 | tf_op jit(solution)/shard_map/all_to_all | solution.py:473
  127.7 0.0 copy-done
  127.7 0.7 slice_bitcast_fusion
  128.4 1.4 collective-permute-start
  129.8 2.1 collective-permute-start.1
  131.9 1.2 collective-permute-start.2
  133.1 0.0 copy-done.2
  133.1 0.7 dynamic-slice.2
  134.5 0.1 pad_add_fusion.flags_ref
  134.5 22.9 %collective-permute-done.first_ref = bf16[144,1024]{1,0:T(8,128)(2,1)S(1)} collective-permute-done((bf16[144,1024]{1,0:T(8,128)(2,1)}, bf16[144,1024]{1,0:T(8,128)(2,1)S(1)}, u32[]{:S(2)}, u32[]{:S(2)}) %collective-permute-start) | collective-permute-done | bytes 294944 | tf_op jit(solution)/shard_map/ppermute | solution.py:464
  157.5 17.9 %collective-permute-done.1.second_ref = bf16[144,1024]{1,0:T(8,128)(2,1)S(1)} collective-permute-done((bf16[144,1024]{1,0:T(8,128)(2,1)}, bf16[144,1024]{1,0:T(8,128)(2,1)S(1)}, u32[]{:S(2)}, u32[]{:S(2)}) %collective-permute-start.1) | collective-permute-done | bytes 294944 | tf_op jit(solution)/shard_map/ppermute | solution.py:464
  175.4 0.0 collective-permute-done.2.third_ref
  175.4 0.0 all-to-all-done.1.parts_ref
  175.4 0.0 copy-done.1
  175.4 1.9 statistic.1
  177.3 36.5 %all_to_all.16.pieces_ref = bf16[4,1152,128]{2,1,0:T(8,128)(2,1)S(1)} all-to-all(bf16[4,1152,128]{2,1,0:T(8,128)(2,1)S(1)} %get-tuple-element.16), channel_id=1, replica_groups=mesh['expert'=64,'group'=4] {'group'}, dimensions={0} | all-to-all | bytes 2359296 | tf_op jit(solution)/shard_map/all_to_all | solution.py:476
  213.8 12.9 %root.1 = (f32[256,1024]{1,0:T(8,128)}, bf16[256,1024]{1,0:T(8,128)(2,1)}, bf16[1024,1024]{1,0:T(8,128)(2,1)}) custom-call(s32[2]{0:T(128)S(1)} %pad_add_fusion.flags_ref, bf16[4,1152,128]{2,1,0:T(8,128)(2,1)S(1)} %all_to_all.16.pieces_ref, bf16[256,1024]{1,0:T(8,128)(2,1)S(1)} %bitcast.14, ...), custom_call_target="tpu_custom_call", output_to_operand_aliasing={{0}: (7, {}), {2}: (6, {})} | custom-call | flops 10737418240 | bytes 8388608 | tf_op jit(solution)/shard_map/root/pallas_call | solution.py:429
Async XLA Ops:
  124.0 3.7 %copy-start = (bf16[1,256,1024]{2,1,0:T(8,128)(2,1)S(1)}, bf16[1,256,1024]{2,1,0:T(8,128)(2,1)}, u32[]{:S(2)}) copy-start(bf16[1,256,1024]{2,1,0:T(8,128)(2,1)} %param.10) | copy-start | bytes 1572868
  124.0 9.1 %copy-start.2 = (s32[64]{0:T(128)S(1)}, s32[64]{0:T(128)}, u32[]{:S(2)}) copy-start(s32[64]{0:T(128)} %param.11) | copy-start | bytes 772
  124.0 51.4 %copy-start.1 = (f32[1,256,1024]{2,1,0:T(8,128)S(1)}, f32[1,256,1024]{2,1,0:T(8,128)}, u32[]{:S(2)}) copy-start(f32[1,256,1024]{2,1,0:T(8,128)} %param.9) | copy-start | bytes 3145732
  124.0 51.4 %all-to-all-start.1 = ((bf16[4,1152,128]{2,1,0:T(8,128)(2,1)}), bf16[4,1152,128]{2,1,0:T(8,128)(2,1)S(1)}, u32[]{:S(2)}, u32[]{:S(2)}) async-start(bf16[4,1152,128]{2,1,0:T(8,128)(2,1)} %get-tuple-element.14), calls=%async_computation.1 | async-start | bytes 2359296 | tf_op jit(solution)/shard_map/all_to_all | solution.py:473
  128.4 29.1 %collective-permute-start = (bf16[144,1024]{1,0:T(8,128)(2,1)}, bf16[144,1024]{1,0:T(8,128)(2,1)S(1)}, u32[]{:S(2)}, u32[]{:S(2)}) collective-permute-start(bf16[144,1024]{1,0:T(8,128)(2,1)} %slice_bitcast_fusion), channel_id=1, source_target_pairs={{0,1},{1,2},{2,3},{3,0},{4,5},{5,6},{6,7},{7,4},{8,9},{9,10},{10,1... | collective-permute-start | bytes 884744 | tf_op jit(solution)/shard_map/ppermute | solution.py:464
  129.8 45.6 %collective-permute-start.1 = (bf16[144,1024]{1,0:T(8,128)(2,1)}, bf16[144,1024]{1,0:T(8,128)(2,1)S(1)}, u32[]{:S(2)}, u32[]{:S(2)}) collective-permute-start(bf16[144,1024]{1,0:T(8,128)(2,1)} %slice_bitcast_fusion), channel_id=1, source_target_pairs={{0,2},{1,3},{2,0},{3,1},{4,6},{5,7},{6,4},{7,5},{8,10},{9,11},{10,... | collective-permute-start | bytes 884744 | tf_op jit(solution)/shard_map/ppermute | solution.py:464
  131.9 43.5 %collective-permute-start.2 = (bf16[144,1024]{1,0:T(8,128)(2,1)}, bf16[144,1024]{1,0:T(8,128)(2,1)}, u32[]{:S(2)}, u32[]{:S(2)}) collective-permute-start(bf16[144,1024]{1,0:T(8,128)(2,1)} %slice_bitcast_fusion), channel_id=1, source_target_pairs={{0,3},{1,0},{2,1},{3,2},{4,7},{5,4},{6,5},{7,6},{8,11},{9,8},{10,9... | collective-permute-start | bytes 884744 | tf_op jit(solution)/shard_map/ppermute | solution.py:464

commit v7 on v6

--- a/solution.py
+++ b/solution.py
@@ -259,9 +259,12 @@
     flags_ref,
     pieces_ref,
     prev_ref,
-    first_ref,
-    second_ref,
-    third_ref,
+    up_1,
+    up_2,
+    up_3,
+    down_1,
+    down_2,
+    down_3,
     grad_hbm,
     part_hbm,
     stat_hbm,
@@ -315,8 +318,15 @@
                 at = slice(2 * B + c * REST, 2 * B + (c + 1) * REST)
                 g_ref[(s + 1) * step - REST : (s + 1) * step, c * B : (c + 1) * B] = pieces_ref[s, at, :]
         g_ref[rows_of(me, step - REST), :] = prev_ref[: step - REST, :]
-        for k, upper_ref in enumerate((first_ref, second_ref, third_ref)):
-            g_ref[rows_of(lax.rem(me - k - 1 + group, group), step - REST), :] = upper_ref[...]
+        for k, (below, above) in enumerate(((up_1, down_1), (up_2, down_2), (up_3, down_3)), 1):
+
+            @pl.when(me >= k)
+            def _():
+                g_ref[rows_of(me - k, step - REST), :] = below[...]
+
+            @pl.when(me + k < group)
+            def _():
+                g_ref[rows_of(me + k, step - REST), :] = above[...]
 
     @pl.when(live != 0)
     def _():
@@ -428,14 +438,14 @@
     anywhere = pl.BlockSpec(memory_space=pl.ANY)
     return pl.pallas_call(
         functools.partial(root_kernel, group),
-        in_specs=[smem()] + [vmem()] * (1 + group) + [anywhere] * 2,
+        in_specs=[smem()] + [vmem()] * (2 * group) + [anywhere] * 2,
         out_specs=(anywhere, anywhere, anywhere),
         out_shape=(
             jax.ShapeDtypeStruct(part.shape, jnp.float32),
             jax.ShapeDtypeStruct(prev.shape, jnp.bfloat16),
             jax.ShapeDtypeStruct(grad.shape, jnp.bfloat16),
         ),
-        input_output_aliases={7: 0, 6: 2},
+        input_output_aliases={10: 0, 9: 2},
         scratch_shapes=[square] * 4
         + [
             pltpu.VMEM((order, order), jnp.float32),
@@ -460,18 +470,23 @@
     live = (jnp.take(owner_map, my_expert) < owners).astype(jnp.int32)
     flags = jnp.stack([me, live])
 
-    def shifted(x, k):
-        return lax.ppermute(x, "group", [(g, (g + k) % group) for g in range(group)])
+    def passed(x, way):
+        pairs = [(g, g + way) for g in range(group) if 0 <= g + way < group]
+        return lax.ppermute(x, "group", pairs)
 
     prev = root_prev[0]
     upper = prev[: prev.shape[0] - REST]
-    uppers = [shifted(upper, k) for k in range(1, group)]
+    ups = [passed(upper, 1)]
+    downs = [passed(upper, -1)]
     sent = dispatch(routing.reshape(1, rows), tokens, cotangent, experts)
     sent = sent.reshape(experts, SLOTS, wide + order)
     got = lax.all_to_all(sent, "expert", 0, 0, tiled=True)
+    for _ in range(2, group):
+        ups.append(passed(ups[-1], 1))
+        downs.append(passed(downs[-1], -1))
+    got, *uppers = lax.optimization_barrier((got, *ups, *downs))
     grad, part = gradient(got.reshape(experts * SLOTS, -1), group, wide, 1.0 / math.sqrt(rows))
     parts = lax.all_to_all(part, "group", 0, 0, tiled=True)
-    parts, *uppers = lax.optimization_barrier((parts, *uppers))
     stat_own, send = new_statistic(flags, parts, stat_prev[0], prev, wide * group)
     pieces = lax.all_to_all(send, "group", 0, 0, tiled=True)
     stat, root_rows, update = inverse_root(flags, pieces, prev, uppers, grad, stat_own)

time: 227 us -> 226 us (level)
  the two profiles are of different devices: /device:TPU:9 before, /device:TPU:20 now
where the time goes in v7:
time: 226 us
  waiting for transfers between devices  129 us (57%)
  starting transfers between devices  34.1 us (15%)
  blocking collectives  30.5 us (13%)
  Pallas kernels  26.1 us (12%)
  local copies, waits for them, and re-layouts  3.61 us (2%)
    ppermute x6, waiting for transfers between devices, passed(): return lax.ppermute(x, 'group', pairs)  104 us
    all_to_all x1, blocking collectives, step_of(): pieces = lax.all_to_all(send, 'group', 0, 0, tiled=True)  30.5 us
    all_to_all x1, waiting for transfers between devices, step_of(): parts = lax.all_to_all(part, 'group', 0, 0, tiled=True)  25.5 us
    ppermute x6, starting transfers between devices, passed(): return lax.ppermute(x, 'group', pairs)  15.6 us
    all_to_all x1, starting transfers between devices, step_of(): got = lax.all_to_all(sent, 'expert', 0, 0, tiled=True)  14.8 us
    pallas_call x1, Pallas kernels, inverse_root(): pl.pallas_call(functools.partial(root_kernel, group), in_specs=[smem()] +...  12.4 us
    pallas_call x1, Pallas kernels, gradient(): pl.pallas_call(functools.partial(gradient_kernel, group, scale), in_specs...  7.05 us
    pallas_call x1, Pallas kernels, dispatch(): pl.pallas_call(functools.partial(dispatch_kernel, experts), in_specs=[any...  4.72 us
  transfers between devices with their start and end apart: 8, of which 5 were waited for; matrix products, arithmetic and copies ran while one was open for 0% of the time, Pallas kernels for 0%

profile of v7, /device:TPU:20, one launch (start us, length us, event | category | flops | bytes accessed | tf_op | source)
XLA Modules:
  0.0 225.5 jit_solution(9964569780135818515)
XLA Ops:
  0.6 4.7 %dispatch.1 = bf16[1024,2048]{1,0:T(8,128)(2,1)} custom-call(s32[1,480]{1,0:T(1,128)} %bitcast.17, bf16[480,1024]{1,0:T(8,128)(2,1)} %tok_hbm.1, bf16[480,1024]{1,0:T(8,128)(2,1)} %sig_hbm.1), custom_call_target="tpu_custom_call" | custom-call | flops 2013265920 | bytes 6291456 | tf_op jit(solution)/shard_map/dispatch/pallas_call | solution.py:89
  5.4 0.0 copy-start
  5.4 14.8 %all-to-all-start = ((bf16[64,16,2048]{2,1,0:T(8,128)(2,1)}), bf16[64,16,2048]{2,1,0:T(8,128)(2,1)}, u32[]{:S(2)}, u32[]{:S(2)}) async-start(bf16[64,16,2048]{2,1,0:T(8,128)(2,1)} %bitcast.15), calls=%async_computation | async-start | bytes 8388608 | tf_op jit(solution)/shard_map/all_to_all | solution.py:483
  20.2 0.0 copy-done
  20.3 2.9 %collective-permute-start = (bf16[144,1024]{1,0:T(8,128)(2,1)S(1)}, bf16[144,1024]{1,0:T(8,128)(2,1)S(1)}, u32[]{:S(2)}, u32[]{:S(2)}) collective-permute-start(bf16[144,1024]{1,0:T(8,128)(2,1)S(1)} %slice_bitcast_fusion), channel_id=1, source_target_pairs={{0,1},{1,2},{2,3},{4,5},{5,6},{6,7},{8,9},{9,10},{10,11},{12,13},{... | collective-permute-start | bytes 884744 | tf_op jit(solution)/shard_map/ppermute | solution.py:475
  23.2 1.3 collective-permute-start.3
  24.5 92.3 %collective-permute-done.up_1 = bf16[144,1024]{1,0:T(8,128)(2,1)S(1)} collective-permute-done((bf16[144,1024]{1,0:T(8,128)(2,1)S(1)}, bf16[144,1024]{1,0:T(8,128)(2,1)S(1)}, u32[]{:S(2)}, u32[]{:S(2)}) %collective-permute-start) | collective-permute-done | bytes 294944 | tf_op jit(solution)/shard_map/ppermute | solution.py:475
  116.9 4.4 %collective-permute-start.1 = (bf16[144,1024]{1,0:T(8,128)(2,1)S(1)}, bf16[144,1024]{1,0:T(8,128)(2,1)S(1)}, u32[]{:S(2)}, u32[]{:S(2)}) collective-permute-start(bf16[144,1024]{1,0:T(8,128)(2,1)S(1)} %collective-permute-done.up_1), channel_id=1, source_target_pairs={{0,1},{1,2},{2,3},{4,5},{5,6},{6,7},{8,9},{9,10},{10,11},{12,13},{... | collective-permute-start | bytes 884744 | tf_op jit(solution)/shard_map/ppermute | solution.py:475
  121.3 0.0 collective-permute-done.3.down_1
  121.3 1.3 collective-permute-start.4
  122.6 4.6 %collective-permute-done.1.up_2 = bf16[144,1024]{1,0:T(8,128)(2,1)S(1)} collective-permute-done((bf16[144,1024]{1,0:T(8,128)(2,1)S(1)}, bf16[144,1024]{1,0:T(8,128)(2,1)S(1)}, u32[]{:S(2)}, u32[]{:S(2)}) %collective-permute-start.1) | collective-permute-done | bytes 294944 | tf_op jit(solution)/shard_map/ppermute | solution.py:475
  127.2 4.4 %collective-permute-start.2 = (bf16[144,1024]{1,0:T(8,128)(2,1)S(1)}, bf16[144,1024]{1,0:T(8,128)(2,1)S(1)}, u32[]{:S(2)}, u32[]{:S(2)}) collective-permute-start(bf16[144,1024]{1,0:T(8,128)(2,1)S(1)} %collective-permute-done.1.up_2), channel_id=1, source_target_pairs={{0,1},{1,2},{2,3},{4,5},{5,6},{6,7},{8,9},{9,10},{10,11},{12,13},{... | collective-permute-start | bytes 884744 | tf_op jit(solution)/shard_map/ppermute | solution.py:475
  131.6 0.0 copy-start.2
  131.6 0.7 copy-done.2
  132.3 0.0 collective-permute-done.4.down_2
  132.3 1.3 collective-permute-start.5
  133.6 0.0 copy-start.4
  133.6 0.7 copy-done.4
  134.3 2.3 %collective-permute-done.2.up_3 = bf16[144,1024]{1,0:T(8,128)(2,1)S(1)} collective-permute-done((bf16[144,1024]{1,0:T(8,128)(2,1)S(1)}, bf16[144,1024]{1,0:T(8,128)(2,1)S(1)}, u32[]{:S(2)}, u32[]{:S(2)}) %collective-permute-start.2) | collective-permute-done | bytes 294944 | tf_op jit(solution)/shard_map/ppermute | solution.py:475
  136.7 0.0 copy-start.6
  136.7 0.7 copy-done.6
  137.4 4.6 %collective-permute-done.5.down_3 = bf16[144,1024]{1,0:T(8,128)(2,1)S(1)} collective-permute-done((bf16[144,1024]{1,0:T(8,128)(2,1)S(1)}, bf16[144,1024]{1,0:T(8,128)(2,1)S(1)}, u32[]{:S(2)}, u32[]{:S(2)}) %collective-permute-start.5) | collective-permute-done | bytes 294944 | tf_op jit(solution)/shard_map/ppermute | solution.py:475
  142.0 0.0 copy-start.8
  142.0 0.7 copy-done.8
  142.7 0.0 all-to-all-done
  142.7 7.1 %gradient.1 = (bf16[1024,1024]{1,0:T(8,128)(2,1)}, bf16[4,1152,128]{2,1,0:T(8,128)(2,1)}) custom-call(bf16[1024,2048]{1,0:T(8,128)(2,1)} %bitcast.5.x_ref), custom_call_target="tpu_custom_call" | custom-call | flops 4294967296 | bytes 10485760 | tf_op jit(solution)/shard_map/gradient/pallas_call | solution.py:156
  149.8 0.0 copy-start.10
  149.8 0.0 copy-start.1
  149.8 3.7 %all-to-all-start.1 = ((bf16[4,1152,128]{2,1,0:T(8,128)(2,1)}), bf16[4,1152,128]{2,1,0:T(8,128)(2,1)S(1)}, u32[]{:S(2)}, u32[]{:S(2)}) async-start(bf16[4,1152,128]{2,1,0:T(8,128)(2,1)} %get-tuple-element.18), calls=%async_computation.1 | async-start | bytes 2359296 | tf_op jit(solution)/shard_map/all_to_all | solution.py:489
  153.5 0.0 copy-done.10
  153.5 0.7 dynamic-slice.2
  154.9 0.1 pad_add_fusion.flags_ref
  154.9 25.5 %all-to-all-done.1.parts_ref = bf16[4,1152,128]{2,1,0:T(8,128)(2,1)S(1)} async-done(((bf16[4,1152,128]{2,1,0:T(8,128)(2,1)}), bf16[4,1152,128]{2,1,0:T(8,128)(2,1)S(1)}, u32[]{:S(2)}, u32[]{:S(2)}) %all-to-all-start.1) | async-done | bytes 1179680 | tf_op jit(solution)/shard_map/all_to_all | solution.py:489
  180.5 0.0 copy-done.1
  180.5 0.0 copy-start.3
  180.5 0.0 copy-start.5
  180.5 0.0 copy-start.7
  180.5 0.0 copy-start.9
  180.5 1.9 statistic.1
  182.4 30.5 %all_to_all.15.pieces_ref = bf16[4,1152,128]{2,1,0:T(8,128)(2,1)S(1)} all-to-all(bf16[4,1152,128]{2,1,0:T(8,128)(2,1)S(1)} %get-tuple-element.19), channel_id=1, replica_groups=mesh['expert'=64,'group'=4] {'group'}, dimensions={0} | all-to-all | bytes 2359296 | tf_op jit(solution)/shard_map/all_to_all | solution.py:491
  212.9 0.0 copy-done.3
  212.9 0.0 copy-done.5
  212.9 0.0 copy-done.7
  212.9 0.0 copy-done.9
  212.9 12.4 %root.1 = (f32[256,1024]{1,0:T(8,128)}, bf16[256,1024]{1,0:T(8,128)(2,1)}, bf16[1024,1024]{1,0:T(8,128)(2,1)}) custom-call(s32[2]{0:T(128)S(1)} %pad_add_fusion.flags_ref, bf16[4,1152,128]{2,1,0:T(8,128)(2,1)S(1)} %all_to_all.15.pieces_ref, bf16[256,1024]{1,0:T(8,128)(2,1)S(1)} %bitcast.13, ...), custom_call_target="tpu_custom_call", output_to_operand_aliasing={{0}: (10, {}), {2}: (9, {})} | custom-call | flops 10737418240 | bytes 8388608 | tf_op jit(solution)/shard_map/root/pallas_call | solution.py:439
  (1 shorter events, 0.0 us)
Async XLA Ops:
  5.4 14.9 %copy-start = (bf16[1,256,1024]{2,1,0:T(8,128)(2,1)S(1)}, bf16[1,256,1024]{2,1,0:T(8,128)(2,1)}, u32[]{:S(2)}) copy-start(bf16[1,256,1024]{2,1,0:T(8,128)(2,1)} %param.10) | copy-start | bytes 1572868
  5.4 137.4 %all-to-all-start = ((bf16[64,16,2048]{2,1,0:T(8,128)(2,1)}), bf16[64,16,2048]{2,1,0:T(8,128)(2,1)}, u32[]{:S(2)}, u32[]{:S(2)}) async-start(bf16[64,16,2048]{2,1,0:T(8,128)(2,1)} %bitcast.15), calls=%async_computation | async-start | bytes 8388608 | tf_op jit(solution)/shard_map/all_to_all | solution.py:483
  20.3 96.6 %collective-permute-start = (bf16[144,1024]{1,0:T(8,128)(2,1)S(1)}, bf16[144,1024]{1,0:T(8,128)(2,1)S(1)}, u32[]{:S(2)}, u32[]{:S(2)}) collective-permute-start(bf16[144,1024]{1,0:T(8,128)(2,1)S(1)} %slice_bitcast_fusion), channel_id=1, source_target_pairs={{0,1},{1,2},{2,3},{4,5},{5,6},{6,7},{8,9},{9,10},{10,11},{12,13},{... | collective-permute-start | bytes 884744 | tf_op jit(solution)/shard_map/ppermute | solution.py:475
  23.2 98.0 %collective-permute-start.3 = (bf16[144,1024]{1,0:T(8,128)(2,1)S(1)}, bf16[144,1024]{1,0:T(8,128)(2,1)S(1)}, u32[]{:S(2)}, u32[]{:S(2)}) collective-permute-start(bf16[144,1024]{1,0:T(8,128)(2,1)S(1)} %slice_bitcast_fusion), channel_id=1, source_target_pairs={{1,0},{2,1},{3,2},{5,4},{6,5},{7,6},{9,8},{10,9},{11,10},{13,12},{... | collective-permute-start | bytes 884744 | tf_op jit(solution)/shard_map/ppermute | solution.py:475
  116.9 10.3 %collective-permute-start.1 = (bf16[144,1024]{1,0:T(8,128)(2,1)S(1)}, bf16[144,1024]{1,0:T(8,128)(2,1)S(1)}, u32[]{:S(2)}, u32[]{:S(2)}) collective-permute-start(bf16[144,1024]{1,0:T(8,128)(2,1)S(1)} %collective-permute-done.up_1), channel_id=1, source_target_pairs={{0,1},{1,2},{2,3},{4,5},{5,6},{6,7},{8,9},{9,10},{10,11},{12,13},{... | collective-permute-start | bytes 884744 | tf_op jit(solution)/shard_map/ppermute | solution.py:475
  121.3 11.0 %collective-permute-start.4 = (bf16[144,1024]{1,0:T(8,128)(2,1)S(1)}, bf16[144,1024]{1,0:T(8,128)(2,1)S(1)}, u32[]{:S(2)}, u32[]{:S(2)}) collective-permute-start(bf16[144,1024]{1,0:T(8,128)(2,1)S(1)} %collective-permute-done.3.down_1), channel_id=1, source_target_pairs={{1,0},{2,1},{3,2},{5,4},{6,5},{7,6},{9,8},{10,9},{11,10},{13,12},{... | collective-permute-start | bytes 884744 | tf_op jit(solution)/shard_map/ppermute | solution.py:475
  127.2 9.5 %collective-permute-start.2 = (bf16[144,1024]{1,0:T(8,128)(2,1)S(1)}, bf16[144,1024]{1,0:T(8,128)(2,1)S(1)}, u32[]{:S(2)}, u32[]{:S(2)}) collective-permute-start(bf16[144,1024]{1,0:T(8,128)(2,1)S(1)} %collective-permute-done.1.up_2), channel_id=1, source_target_pairs={{0,1},{1,2},{2,3},{4,5},{5,6},{6,7},{8,9},{9,10},{10,11},{12,13},{... | collective-permute-start | bytes 884744 | tf_op jit(solution)/shard_map/ppermute | solution.py:475
  131.6 0.7 copy-start.2
  132.3 9.7 %collective-permute-start.5 = (bf16[144,1024]{1,0:T(8,128)(2,1)S(1)}, bf16[144,1024]{1,0:T(8,128)(2,1)S(1)}, u32[]{:S(2)}, u32[]{:S(2)}) collective-permute-start(bf16[144,1024]{1,0:T(8,128)(2,1)S(1)} %collective-permute-done.4.down_2), channel_id=1, source_target_pairs={{1,0},{2,1},{3,2},{5,4},{6,5},{7,6},{9,8},{10,9},{11,10},{13,12},{... | collective-permute-start | bytes 884744 | tf_op jit(solution)/shard_map/ppermute | solution.py:475
  133.6 0.7 copy-start.4
  136.7 0.7 copy-start.6
  142.0 0.7 copy-start.8
  149.8 3.7 %copy-start.10 = (s32[64]{0:T(128)S(1)}, s32[64]{0:T(128)}, u32[]{:S(2)}) copy-start(s32[64]{0:T(128)} %param.11) | copy-start | bytes 772
  149.8 30.7 %copy-start.1 = (f32[1,256,1024]{2,1,0:T(8,128)S(1)}, f32[1,256,1024]{2,1,0:T(8,128)}, u32[]{:S(2)}) copy-start(f32[1,256,1024]{2,1,0:T(8,128)} %param.9) | copy-start | bytes 3145732
  149.8 30.6 %all-to-all-start.1 = ((bf16[4,1152,128]{2,1,0:T(8,128)(2,1)}), bf16[4,1152,128]{2,1,0:T(8,128)(2,1)S(1)}, u32[]{:S(2)}, u32[]{:S(2)}) async-start(bf16[4,1152,128]{2,1,0:T(8,128)(2,1)} %get-tuple-element.18), calls=%async_computation.1 | async-start | bytes 2359296 | tf_op jit(solution)/shard_map/all_to_all | solution.py:489
  180.5 32.4 %copy-start.3 = (bf16[144,1024]{1,0:T(8,128)(2,1)S(1)}, bf16[144,1024]{1,0:T(8,128)(2,1)}, u32[]{:S(2)}) copy-start(bf16[144,1024]{1,0:T(8,128)(2,1)} %copy-done.2) | copy-start | bytes 884740
  180.5 32.4 %copy-start.5 = (bf16[144,1024]{1,0:T(8,128)(2,1)S(1)}, bf16[144,1024]{1,0:T(8,128)(2,1)}, u32[]{:S(2)}) copy-start(bf16[144,1024]{1,0:T(8,128)(2,1)} %copy-done.4) | copy-start | bytes 884740
  180.5 32.4 %copy-start.7 = (bf16[144,1024]{1,0:T(8,128)(2,1)S(1)}, bf16[144,1024]{1,0:T(8,128)(2,1)}, u32[]{:S(2)}) copy-start(bf16[144,1024]{1,0:T(8,128)(2,1)} %copy-done.6) | copy-start | bytes 884740
  180.5 32.4 %copy-start.9 = (bf16[144,1024]{1,0:T(8,128)(2,1)S(1)}, bf16[144,1024]{1,0:T(8,128)(2,1)}, u32[]{:S(2)}) copy-start(bf16[144,1024]{1,0:T(8,128)(2,1)} %copy-done.8) | copy-start | bytes 884740
